TPU v7x, 128 devices: a whole 4x4x4 slice. The times are simulated.
128 devices in a mesh: ops: 32 (over z, y, core), site: 4 (over x).
Axes of the slice: x: 4, y: 4, z: 4, core: 2. Of those that a mesh axis runs over, the one named last changes fastest.
Arguments:
- wavefunction: bfloat16 [2048, 2048], replicated, may hold values from -6 to 6
- left_blocks: bfloat16 [256, 16, 192, 192], P('ops', 'site'), may hold values from -0.4375 to 0.4375
- right_blocks: bfloat16 [256, 16, 192, 192], P('ops', 'site'), may hold values from -0.078125 to 0.078125
- left_sector: int32 [2048], replicated, may hold values from 0 to 15, as said below
- right_sector: int32 [2048], replicated, may hold values from 0 to 15, as said below
- term_count: int32 [32], P('ops'), may hold values from 1 to 8, as said below
- left_energy: float32 [2048], replicated, may hold values from -1 to 1
- right_energy: float32 [2048], replicated, may hold values from -1 to 1
- subspace: bfloat16 [2, 16, 192, 2048], P(None, 'site'), may hold values from -0.0078125 to 0.0078125
Outputs:
- sigma: bfloat16 [16, 192, 2048], P('site')
- projections: float32 [2], replicated
Inputs may be any that keep to these rules, and one draw needn't show every extreme that they name: `left_sector`: sector ids never fall along the bond; each of the 16 sectors has 1 to 192 states and one has exactly 192. `right_sector`: sector ids never fall along the bond; each of the 16 sectors has 1 to 192 states and one has exactly 192. `term_count`: some group has all 8 slots live.
All inputs are finite; a program needn't handle non-finite values.
Results may differ from a plain program's by a relative error of at most 0.0045.
Values may be sent and summed in bfloat16 or wider, within the bound.
A program may use at most 192 MiB of HBM per device.

v0:
```python
import jax
import jax.numpy as jnp
from jax import lax
from jax.sharding import PartitionSpec as P


def from_everyone(value, axis):
    size = lax.axis_size(axis)
    return lax.all_to_all(
        jnp.broadcast_to(value[None], (size, *value.shape)), axis, 0, 0, tiled=True
    )


def over_copies(value, axis):
    return from_everyone(value, axis).sum(axis=0)


def sector_tables(sector_ids, sectors):
    labels = jnp.arange(sectors, dtype=jnp.int32)
    sector_starts = jnp.sum((sector_ids[None, :] < labels[:, None]).astype(jnp.int32), axis=1)
    sector_sizes = jnp.sum((sector_ids[None, :] == labels[:, None]).astype(jnp.int32), axis=1)
    return (sector_starts, sector_sizes)


def block_mask(size_now, widest):
    inside = jnp.arange(widest, dtype=jnp.int32) < size_now
    return inside[:, None] & inside[None, :]


def correlations(vectors, values):
    return jnp.sum(vectors.astype(jnp.float32) * values[None], axis=(1, 2, 3))


def local(
    wavefunction,
    left_blocks,
    right_blocks,
    left_sector,
    right_sector,
    term_count,
    left_energy,
    right_energy,
    subspace,
):
    slot_count = left_blocks.shape[0]
    sec_dev = left_blocks.shape[1]
    widest = left_blocks.shape[2]
    bond_dim = wavefunction.shape[0]
    row_count = sec_dev * widest
    sectors = sec_dev * lax.axis_size("site")
    left_start, left_size = sector_tables(left_sector, sectors)
    right_start, right_size = sector_tables(right_sector, sectors)
    active = term_count[0]
    first_sector = lax.axis_index("site") * sec_dev
    psi_padded = jnp.concatenate(
        [wavefunction, jnp.zeros((widest, bond_dim), wavefunction.dtype)], axis=0
    )
    energy_padded = jnp.concatenate([left_energy, jnp.zeros((widest,), jnp.float32)])
    psi_slabs = []
    energies = []
    left_masks = []
    inside_rows = []
    for within in range(sec_dev):
        sector = first_sector + within
        row_start = left_start[sector]
        size_now = left_size[sector]
        psi_slabs.append(lax.dynamic_slice_in_dim(psi_padded, row_start, widest, 0))
        energies.append(lax.dynamic_slice_in_dim(energy_padded, row_start, widest, 0))
        inside = jnp.arange(widest, dtype=jnp.int32) < size_now
        inside_rows.append(inside)
        left_masks.append(inside[:, None] & inside[None, :])

    def left_term(term_idx, stacked):
        blocks = lax.dynamic_index_in_dim(left_blocks, term_idx, 0, False)
        pieces = []
        for within in range(sec_dev):
            masked = jnp.where(left_masks[within], blocks[within], jnp.zeros((), blocks.dtype))
            pieces.append(jnp.dot(masked, psi_slabs[within], preferred_element_type=jnp.float32))
        left_image = jnp.concatenate(pieces, axis=0).astype(jnp.bfloat16)
        left_image = jnp.concatenate(
            [left_image, jnp.zeros((row_count, widest), jnp.bfloat16)], axis=1
        )
        return lax.dynamic_update_index_in_dim(stacked, left_image, term_idx, 0)

    images = lax.fori_loop(
        0, active, left_term, jnp.zeros((slot_count, row_count, bond_dim + widest), jnp.bfloat16)
    )
    part_blocks = lax.all_gather(right_blocks, "site", axis=1, tiled=True)

    def one_sector(within, summed):
        col_start = right_start[within]
        keep_mask = block_mask(right_size[within], widest)
        blocks = lax.dynamic_index_in_dim(part_blocks, within, 1, False)

        def add_term(term_idx, running):
            window = lax.dynamic_slice_in_dim(
                lax.dynamic_index_in_dim(images, term_idx, 0, False), col_start, widest, 1
            )
            one_block = jnp.where(
                keep_mask,
                lax.dynamic_index_in_dim(blocks, term_idx, 0, False),
                jnp.zeros((), blocks.dtype),
            )
            return running + lax.dot_general(
                window, one_block, (((1,), (1,)), ((), ())), preferred_element_type=jnp.float32
            )

        added = lax.fori_loop(0, active, add_term, jnp.zeros((row_count, widest), jnp.float32))
        previous = lax.dynamic_slice_in_dim(summed, col_start, widest, 1)
        return lax.dynamic_update_slice_in_dim(summed, previous + added, col_start, 1)

    folded = lax.fori_loop(
        0, part_blocks.shape[1], one_sector, jnp.zeros((row_count, bond_dim + widest), jnp.float32)
    )
    partial_value = folded[:, :bond_dim].reshape(sec_dev, widest, bond_dim)
    psi_mine = jnp.where(
        jnp.stack(inside_rows)[:, :, None],
        jnp.stack(psi_slabs).astype(jnp.float32),
        jnp.float32(0.0),
    )
    energy_mine = jnp.stack(energies)
    diagonal = (energy_mine[:, :, None] + right_energy[None, None, :]) * psi_mine
    sigma_full = lax.psum(partial_value, "ops") + diagonal
    sigma_out = sigma_full.astype(jnp.bfloat16)
    projections = over_copies(correlations(subspace, sigma_full), "site")
    return (sigma_out, projections)


def solution(mesh):
    in_specs = (
        P(),
        P("ops", "site", None, None),
        P("ops", "site", None, None),
        P(),
        P(),
        P("ops"),
        P(),
        P(),
        P(None, "site", None, None),
    )
    out_specs = (P("site", None, None), P())
    return jax.shard_map(local, mesh=mesh, in_specs=in_specs, out_specs=out_specs, check_vma=False)
```

profile of v0, /device:TPU:1, one launch (start us, length us, event | category | flops | bytes accessed | tf_op | source)
XLA Modules:
  0.0 716.9 jit_solution(18417771134688194427)
XLA Ops:
  7.2 3.9 copy.17
  22.2 5.3 pad_dynamic-slice_fusion
  27.4 10.2 %broadcast_in_dim.39 = bf16[8,768,2240]{2,1,0:T(8,128)(2,1)} broadcast(bf16[]{:T(256)} %constant.184.clone.1), dimensions={} | broadcast | bytes 27525122 | tf_op jit(solution)/shard_map/broadcast_in_dim | solution.py:86
  37.7 30.2 %while.63 = (s32[]{:T(128)}, bf16[8,768,2240]{2,1,0:T(8,128)(2,1)}, s32[]{:T(128)}, bf16[8,4,192,192]{3,2,1,0:T(8,128)(2,1)}, bf16[192,2048]{1,0:T(8,128)(2,1)},...) while((s32[]{:T(128)}, bf16[8,768,2240]{2,1,0:T(8,128)(2,1)}, ...), condition=%wide.region_5.6_spmd.clone, body=%wide.region_4.5_spmd.clone.sunk | while | flops 628211712 | bytes 13373707 | solution.py:85
  44.2 3.2 fusion.67
  54.0 3.3 fusion.67
  63.8 3.4 fusion.67
  67.8 65.0 %all-gather.2.cloned.1.call-done = bf16[8,16,192,192]{3,2,0,1:T(8,128)(2,1)} async-done(((bf16[8,4,192,192]{3,2,0,1:T(8,128)(2,1)}), bf16[8,16,192,192]{3,2,0,1:T(8,128)(2,1)}) %all-gather.2.cloned.1.call-update) | async-done | bytes 9437200 | tf_op jit(solution)/shard_map/all_gather | solution.py:88
  132.8 3.3 broadcast_in_dim.38
  136.2 258.5 %while.62 = (s32[]{:T(128)}, f32[768,2240]{0,1:T(8,128)}, s32[16]{0:T(128)S(1)}, bf16[8,16,192,192]{3,2,0,1:T(8,128)(2,1)}, s32[16]{0:T(128)S(1)}, /*index=5*/s3...) while((s32[]{:T(128)}, f32[768,2240]{0,1:T(8,128)}, ...), condition=%wide.region_9.10_spmd, body=%wide.region_6.9_spmd.sunk | while | flops 56991944 | bytes 6391994 | solution.py:112
  141.2 7.0 while.64
  149.4 3.0 dynamic_update_slice.19
  157.3 7.0 while.64
  165.5 3.0 dynamic_update_slice.19
  173.5 7.0 while.64
  181.7 3.0 dynamic_update_slice.19
  189.7 7.0 while.64
  197.8 3.0 dynamic_update_slice.19
  205.8 7.0 while.64
  214.0 2.9 dynamic_update_slice.19
  222.0 7.0 while.64
  230.2 3.0 dynamic_update_slice.19
  238.1 7.0 while.64
  246.3 3.0 dynamic_update_slice.19
  254.3 7.0 while.64
  262.5 3.0 dynamic_update_slice.19
  270.5 7.0 while.64
  278.6 3.0 dynamic_update_slice.19
  286.6 7.0 while.64
  294.8 3.0 dynamic_update_slice.19
  302.8 7.0 while.64
  311.0 3.0 dynamic_update_slice.19
  319.0 7.0 while.64
  327.1 3.0 dynamic_update_slice.19
  335.1 7.0 while.64
  343.3 3.0 dynamic_update_slice.19
  351.3 7.0 while.64
  359.4 2.9 dynamic_update_slice.19
  367.4 7.0 while.64
  375.6 3.0 dynamic_update_slice.19
  383.5 7.0 while.64
  391.7 2.9 dynamic_update_slice.19
  394.7 5.8 slice.19
  400.5 6.6 copy.18
  410.0 282.4 %all-reduce.5.cloned.1.call-done = f32[4,192,2048]{2,1,0:T(8,128)} async-done(((f32[4,192,2048]{2,1,0:T(8,128)}), f32[4,192,2048]{2,1,0:T(8,128)}) %all-reduce.5.cloned.1.call-update) | async-done | bytes 6291472 | tf_op jit(solution)/shard_map/psum | solution.py:123
  692.4 4.7 fusion.49
  697.0 4.6 multiply_reduce_fusion
  701.6 7.9 %all_to_all.6 = f32[4,1,2]{2,1,0:T(1,128)S(1)} all-to-all(f32[4,1,2]{2,1,0:T(1,128)S(1)} %broadcast_in_dim.42), channel_id=1, replica_groups=mesh['ops'=32,'site'=4] {'site'}, dimensions={0} | all-to-all | bytes 64 | tf_op jit(solution)/shard_map/all_to_all | solution.py:9
  (188 shorter events, 161.1 us)
Async XLA Ops:
  7.2 4.0 copy-start.4
  7.2 14.8 %copy-start.5 = (s32[2048]{0:T(1024)S(1)}, s32[2048]{0:T(1024)}, u32[]{:S(2)}) copy-start(s32[2048]{0:T(1024)} %param.19) | copy-start | bytes 24580
  7.2 125.7 %all-gather.2.cloned.1.call-start = ((), (), s32[]{:S(2)}) async-start(), calls=%async_computation.1 | async-start | bytes 15728640 | tf_op jit(solution)/shard_map/all_gather | solution.py:88
  11.1 681.2 %all-reduce.5.cloned.1.call-start = ((), (), s32[]{:S(2)}) async-start(), calls=%async_computation.2 | async-start | bytes 12582912 | tf_op jit(solution)/shard_map/psum | solution.py:123
  407.2 2.7 copy-start.3
  407.2 285.2 %copy-start = (bf16[192,2048]{1,0:T(8,128)(2,1)S(1)}, bf16[192,2048]{1,0:T(8,128)(2,1)}, u32[]{:S(2)}) copy-start(bf16[192,2048]{1,0:T(8,128)(2,1)} %get-tuple-element.834) | copy-start | bytes 2359300
  407.2 285.2 %copy-start.1 = (bf16[192,2048]{1,0:T(8,128)(2,1)S(1)}, bf16[192,2048]{1,0:T(8,128)(2,1)}, u32[]{:S(2)}) copy-start(bf16[192,2048]{1,0:T(8,128)(2,1)} %get-tuple-element.835) | copy-start | bytes 2359300
  407.2 285.2 %copy-start.2 = (f32[2048]{0:T(1024)S(1)}, f32[2048]{0:T(1024)}, u32[]{:S(2)}) copy-start(f32[2048]{0:T(1024)} %param.22) | copy-start | bytes 24580
Sparse Core Ops, SparseCore 0:
  11.3 121.5 all-gather.1
  407.3 284.9 all-reduce.4
where the time goes:
time: 728 us; the launch traced here: 717 us
  waiting for transfers between devices  347 us (48%)
  local copies, waits for them, and re-layouts  122 us (17%)
  matrix products  87 us (12%)
  loops' own time  77.2 us (11%)
  other arithmetic  53.9 us (7%)
  between operations  21.6 us (3%)
  blocking collectives  7.89 us (1%)
    psum x1, waiting for transfers between devices, local(): sigma_full = lax.psum(partial_value, 'ops') + diagonal  282 us
    dot_general x48, matrix products, add_term(): lax.dot_general(window, one_block, (((1,), (1,)), ((), ())), preferred_el...  69.4 us
    all_gather x1, waiting for transfers between devices, local(): part_blocks = lax.all_gather(right_blocks, 'site', axis=1, tiled=True)  65 us
    dynamic_update_slice x16, local copies, waits for them, and re-layouts, one_sector(): lax.dynamic_update_slice_in_dim(summed, previous + added, col_start, 1)  47.4 us
    another operation x16, loops' own time, one_sector(): lax.fori_loop(0, active, add_term, jnp.zeros((row_count, widest), jnp.flo...  42.8 us
    another operation x1, loops' own time, local(): lax.fori_loop(0, part_blocks.shape[1], one_sector, jnp.zeros((row_count,...  31.6 us
    squeeze x16, local copies, waits for them, and re-layouts, one_sector(): blocks = lax.dynamic_index_in_dim(part_blocks, within, 1, False)  19.1 us
    add x16, other arithmetic, one_sector(): previous + added  18.4 us
  transfers between devices with their start and end apart: 2, of which 2 were waited for; matrix products, arithmetic and copies ran while one was open for 7% of the time, Pallas kernels for 0%

commit v1 on v0

v1 whole, which is shorter than its diff:
```python
import jax
import jax.numpy as jnp
from jax import lax
from jax.experimental import pallas as pl
from jax.experimental.pallas import tpu as pltpu
from jax.sharding import PartitionSpec as P

W = 192
SLOTS = 8
NS = 2
NC = SLOTS // NS
BOND = 2048
BF = jnp.bfloat16
F32 = jnp.float32
MESH = pl.DeviceIdType.MESH


def iota(shape, dim):
    return lax.broadcasted_iota(jnp.int32, shape, dim)


def one_hot(mask):
    return jnp.where(mask, F32(1), F32(0)).astype(BF)


def packed_index(pos, parity):
    tail = pos - 64 * parity
    idx = jnp.where(pos < 128, pos, tail)
    ok = (pos < 128) | ((tail >= 128) & (tail < W))
    return idx, ok


def piece_offsets(bits):
    offs = []
    for qi in range(4):
        off = [0]
        for s in range(4):
            off.append(off[-1] + bits[(qi + s) % 4] * (384 >> s))
        offs.append(off)
    return offs


def label_bits(y, z):
    return (((y + 1) // 2) % 2, ((z + 1) // 2) % 2, y // 2, z // 2)


def prep_body(
    lstart, lsize, rstart, rsize, psi_v, lenergy, renergy, sub_hbm,
    pp_hbm, diag, subp, gath, pp, stack, sub_sem, pp_sem,
):
    x = lax.axis_index("site")
    o = lax.axis_index("ops")
    c = o % 2
    x_l = x + 1 - 2 * (x % 2)
    x_r = 3 - x
    offs = piece_offsets(label_bits((o // 2) % 4, o // 8))

    def sub_copy(qi, k):
        off = offs[qi][4]
        return pltpu.make_async_copy(
            sub_hbm.at[k, off // W, pl.ds(pl.multiple_of(off % W, 16), 48), :],
            stack.at[qi, pl.ds(48 + 48 * k, 48), :], sub_sem.at[qi, k])

    for qi in range(4):
        for k in range(2):
            sub_copy(qi, k).start()

    def row_hot(q, first, rows, packed):
        rs = lstart[q]
        base = pl.multiple_of(jnp.minimum((rs // 16) * 16, BOND - 256), 16)
        pos = iota((rows, 256), 0) + first
        if packed:
            idx, ok = packed_index(pos, q % 2)
        else:
            idx, ok = pos, pos < W
        ok = ok & (idx < lsize[q])
        return base, one_hot(ok & (iota((rows, 256), 1) == idx + (rs - base)))

    def rows_of(i, carry):
        q = jnp.where(i < 4, x * 4 + i, x_l * 4 + i - 4)
        base, hot = row_hot(q, 0, 256, True)
        for n in range(4):
            win = psi_v[pl.ds(base, 256), pl.ds(n * 512, 512)]
            gath[pl.ds(pl.multiple_of(i * 256, 256), 256), pl.ds(n * 512, 512)] = jnp.dot(
                hot, win, preferred_element_type=F32).astype(BF)
        return carry

    lax.fori_loop(0, 8, rows_of, 0)

    def pp_copy(j):
        return pltpu.make_async_copy(pp.at[j], pp_hbm.at[j], pp_sem.at[j])

    def cols_of(j, carry):
        q = jnp.where(j < 4, x * 4 + j, x_r * 4 + j - 4)
        cs = rstart[q]
        cb = pl.multiple_of(jnp.minimum((cs // 128) * 128, BOND - 384), 128)
        idx, ok = packed_index(iota((384, 256), 1), q % 2)
        ok = ok & (idx < rsize[q])
        hot = one_hot(ok & (iota((384, 256), 0) == idx + (cs - cb)))
        for m in range(4):
            win = gath[pl.ds(m * 512, 512), pl.ds(cb, 384)]
            pp[j, pl.ds(m * 512, 512), :] = jnp.dot(win, hot, preferred_element_type=F32).astype(BF)
        pp_copy(j).start()
        return carry

    lax.fori_loop(0, 8, cols_of, 0)

    re = renergy[...]
    hi = re.astype(BF)
    rem = re - hi.astype(F32)
    mid = rem.astype(BF)
    low = (rem - mid.astype(F32)).astype(BF)
    rows16 = iota((16, BOND), 0)
    er3 = jnp.where(rows16 == 0, hi.astype(F32),
                    jnp.where(rows16 == 1, mid.astype(F32),
                              jnp.where(rows16 == 2, low.astype(F32), F32(0)))).astype(BF)
    for qi in range(4):
        l2, t = qi // 2, qi % 2
        off = offs[qi][4]
        q = x * 4 + off // W
        a0 = off % W
        base, hot = row_hot(q, a0, 48, False)
        for n in range(4):
            win = psi_v[pl.ds(base, 256), pl.ds(n * 512, 512)]
            stack[qi, pl.ds(0, 48), pl.ds(n * 512, 512)] = jnp.dot(
                hot, win, preferred_element_type=F32).astype(BF)
        stack[qi, pl.ds(144, 16), :] = er3
        for k in range(2):
            sub_copy(qi, k).wait()
        xt = x if t == 0 else x_l
        site = xt + c * (3 - 2 * xt)
        total = None
        for par in range(2):
            qr = site * 4 + 2 * l2 + par
            cs = rstart[qr]
            cb = pl.multiple_of(jnp.minimum((cs // 128) * 128, BOND - 384), 128)
            j = iota((384, 384), 1) - W * par
            hot2 = one_hot((j >= 0) & (j < W) & (j < rsize[qr]) & (iota((384, 384), 0) == j + (cs - cb)))
            part = jnp.dot(stack[qi, :, pl.ds(cb, 384)], hot2, preferred_element_type=F32)
            total = part if total is None else total + part
        lb = pl.multiple_of(jnp.minimum((lstart[q] // 128) * 128, BOND - 384), 128)
        shift = lstart[q] - lb + a0
        pick = iota((48, 384), 1) == iota((48, 384), 0) + shift
        el = jnp.sum(jnp.where(pick, lenergy[:, pl.ds(lb, 384)], F32(0)), axis=1, keepdims=True)
        er = total[144:145] + total[145:146] + total[146:147]
        diag[qi] = (el + er) * total[:48]
        subp[qi, 0] = total[48:96]
        subp[qi, 1] = total[96:144]

    for j in range(8):
        pp_copy(j).wait()


def body(
    lsize, count, pp_hbm, left_hbm, right_hbm, diag, subp,
    out_hbm, proj_out,
    slabs_v, pp, raw, lown, lfor, rown, rfor, li, acc,
    drecv, rs0, rs1, rs2, rs3, xrecv, pvs, pvr,
    raw_sem, pp_sem, out_sem,
    l_ss, l_rs, r_ss, r_rs, d_ss, d_rs, rs_ss, rs_rs, x_ss, x_rs,
    ag_ss, ag_rs, fw_ss, fw_rs, pv_ss, pv_rs,
):
    x = lax.axis_index("site")
    o = lax.axis_index("ops")
    c = o % 2
    y = (o // 2) % 4
    z = o // 8
    x_l = x + 1 - 2 * (x % 2)
    x_r = 3 - x
    to_l = {"site": x_l}
    to_r = {"site": x_r}
    sib = {"ops": o + 1 - 2 * c}
    y_a = y + 1 - 2 * (y % 2)
    z_a = z + 1 - 2 * (z % 2)
    dims = (
        {"ops": o + 2 * (y_a - y)},
        {"ops": o + 8 * (z_a - z)},
        {"ops": o + 2 * (3 - 2 * y)},
        {"ops": o + 8 * (3 - 2 * z)},
    )
    bits = label_bits(y, z)

    def raw_copies(ch):
        buf = ch % 2
        return (
            pltpu.make_async_copy(left_hbm.at[pl.ds(NS * ch, NS)], raw.at[buf, 0], raw_sem.at[buf, 0]),
            pltpu.make_async_copy(right_hbm.at[pl.ds(NS * ch, NS)], raw.at[buf, 1], raw_sem.at[buf, 1]),
        )

    for ch in range(2):
        for cp in raw_copies(ch):
            cp.start()
    pp_copy = pltpu.make_async_copy(pp_hbm, pp, pp_sem)
    pp_copy.start()
    offs = piece_offsets(bits)

    barrier = pltpu.get_barrier_semaphore()
    for who in (to_l, to_r, sib, *dims):
        pl.semaphore_signal(barrier, inc=1, device_id=who, device_id_type=MESH)

    zrow = jnp.zeros((NC, NS, 2, 3, 64, 128), BF)
    for buf in (rown, rfor):
        for start in (0, 256):
            buf[:, :, :, :, pl.ds(start, 64), :] = zrow

    def l_copy(ch):
        return pltpu.make_async_remote_copy(
            src_ref=lown.at[ch], dst_ref=lfor.at[ch], send_sem=l_ss.at[ch], recv_sem=l_rs.at[ch],
            device_id=to_l, device_id_type=MESH)

    def r_copy(ch):
        rows = pl.ds(64, W)
        return pltpu.make_async_remote_copy(
            src_ref=rown.at[ch, :, :, :, rows, :], dst_ref=rfor.at[ch, :, :, :, rows, :],
            send_sem=r_ss.at[ch], recv_sem=r_rs.at[ch], device_id=to_r, device_id_type=MESH)

    def pack(ch):
        buf = ch % 2

        def one(k, carry):
            s = k // 2
            p = k % 2
            row = iota((W, 128), 0)
            live = NS * ch + s < count[0]
            keep = []
            for par in range(2):
                size = jnp.where(live, lsize[x * 4 + 2 * p + par], 0)
                keep.append(one_hot(row < size))
            ev = raw[buf, 0, s, 2 * p]
            od = raw[buf, 0, s, 2 * p + 1]
            lown[ch, s, p, 0] = ev[:, :128] * keep[0]
            lown[ch, s, p, 1] = od[:, :128] * keep[1]
            lown[ch, s, p, 2] = jnp.concatenate(
                [ev[:, 128:] * keep[0][:, :64], od[:, 128:] * keep[1][:, :64]], axis=1)
            ev = raw[buf, 1, s, 2 * p]
            od = raw[buf, 1, s, 2 * p + 1]
            rows = pl.ds(64, W)
            rown[ch, s, p, 0, rows, :] = ev[:, :128]
            rown[ch, s, p, 1, rows, :] = od[:, :128]
            rown[ch, s, p, 2, rows, :] = jnp.concatenate([ev[:, 128:], od[:, 128:]], axis=1)
            return carry

        lax.fori_loop(0, 2 * NS, one, 0)

    for ch in range(NC):
        for cp in raw_copies(ch):
            cp.wait()
        pack(ch)
        if ch == 0:
            pl.semaphore_wait(barrier, 7)
        if ch + 2 < NC:
            for cp in raw_copies(ch + 2):
                cp.start()
        l_copy(ch).start()
        r_copy(ch).start()

    pp_copy.wait()

    def clear(r, carry):
        for a in range(2):
            for b in range(2):
                acc[a, b, pl.ds(pl.multiple_of(r * 192, 192), 192), :] = jnp.zeros((192, 384), F32)
        return carry

    lax.fori_loop(0, 8, clear, 0)

    def rectangle(ch, lsrc, rsrc, h, g):
        def pair(p, carry):
            for par in range(2):
                j = g * 4 + 2 * p + par
                for i in range(4):
                    lhs = jnp.concatenate(
                        [lsrc[ch, :, i // 2, i % 2].reshape(NS * W, 128),
                         lsrc[ch, :, i // 2, 2].reshape(NS * W, 128)], axis=1)
                    img = jnp.dot(lhs, pp[j, pl.ds((h * 4 + i) * 256, 256), :],
                                  preferred_element_type=F32).astype(BF)
                    for s in range(NS):
                        li[pl.ds(i * W, W), pl.ds(s * 256, 256)] = img[s * W:(s + 1) * W]
                rows = pl.ds(64 - 64 * par, 256)
                rhs = jnp.concatenate(
                    [rsrc[ch, s, p, k, rows, :] for s in range(NS) for k in (par, 2)], axis=1)
                lanes = pl.ds(128 * par, 256)
                hr = pl.ds(h * 768, 768)
                acc[g, p, hr, lanes] += lax.dot_general(
                    li[...], rhs, (((1,), (1,)), ((), ())), preferred_element_type=F32)
            return carry

        lax.fori_loop(0, 2, pair, 0)

    def chunk(ch, carry):
        rectangle(ch, lown, rown, 0, 0)
        l_copy(ch).wait()
        r_copy(ch).wait()
        rectangle(ch, lfor, rown, 1, 0)
        rectangle(ch, lown, rfor, 0, 1)
        rectangle(ch, lfor, rfor, 1, 1)
        return carry

    lax.fori_loop(0, NC, chunk, 0)

    def d_copy(qi):
        l2, h = qi // 2, qi % 2
        rows = pl.ds(h * 768, 768)
        return pltpu.make_async_remote_copy(
            src_ref=acc.at[1 - c, l2, rows, :], dst_ref=drecv.at[l2, rows, :],
            send_sem=d_ss.at[qi], recv_sem=d_rs.at[qi], device_id=sib, device_id_type=MESH)

    rsb = (rs0, rs1, rs2, rs3)

    def rs_copy(qi, s):
        l2, h = qi // 2, qi % 2
        half = 384 >> s
        d = (qi + s) % 4
        send = offs[qi][s] + (1 - bits[d]) * half
        return pltpu.make_async_remote_copy(
            src_ref=acc.at[c, l2, pl.ds(pl.multiple_of(h * 768 + send, 16), half), :],
            dst_ref=rsb[s].at[qi], send_sem=rs_ss.at[qi, s], recv_sem=rs_rs.at[qi, s],
            device_id=dims[d], device_id_type=MESH)

    def add_rows(l2, first, src, src_first, rows):
        def step(k, carry):
            at = pl.ds(pl.multiple_of(first + k * 48, 16), 48)
            acc[c, l2, at, :] += src[pl.ds(pl.multiple_of(src_first + k * 48, 16), 48), :]
            return carry

        lax.fori_loop(0, rows // 48, step, 0)

    for qi in range(4):
        d_copy(qi).start()
    for qi in range(4):
        l2, h = qi // 2, qi % 2
        d_copy(qi).wait_recv()
        b = bits[qi]
        there = h * 768 + (1 - b) * 384
        here = h * 768 + b * 384
        add_rows(l2, there, drecv.at[l2], there, 384)
        rs_copy(qi, 0).start()
        add_rows(l2, here, drecv.at[l2], here, 384)

    def x_copy(l2):
        off = offs[l2 * 2 + 1][4]
        return pltpu.make_async_remote_copy(
            src_ref=acc.at[c, l2, pl.ds(pl.multiple_of(768 + off, 16), 48), :], dst_ref=xrecv.at[l2],
            send_sem=x_ss.at[l2], recv_sem=x_rs.at[l2], device_id=to_l, device_id_type=MESH)

    for s in range(4):
        for qi in range(4):
            l2, h = qi // 2, qi % 2
            rs_copy(qi, s).wait_recv()
            add_rows(l2, h * 768 + offs[qi][s + 1], rsb[s].at[qi], 0, 384 >> s)
            if s < 3:
                rs_copy(qi, s + 1).start()
            elif h == 1:
                x_copy(l2).start()

    def slab_rows(k, first, rows):
        return slabs_v.at[k, pl.ds(pl.multiple_of(first, 16), rows), :]

    def slab(qi):
        return (qi % 2) * 4 + c * 2 + qi // 2

    def ag_copy(qi, s):
        half = 384 >> s
        d = (qi + s) % 4
        ref = slab_rows(slab(qi), offs[qi][s + 1], half)
        return pltpu.make_async_remote_copy(
            src_ref=ref, dst_ref=ref, send_sem=ag_ss.at[qi, s], recv_sem=ag_rs.at[qi, s],
            device_id=dims[d], device_id_type=MESH)

    def fw_copy(qi, s):
        if s == 4:
            first, rows = offs[qi][4], 48
        else:
            rows = 384 >> s
            first = offs[qi][s] + (1 - bits[(qi + s) % 4]) * rows
        ref = slab_rows(slab(qi), first, rows)
        return pltpu.make_async_remote_copy(
            src_ref=ref, dst_ref=ref, send_sem=fw_ss.at[qi, s], recv_sem=fw_rs.at[qi, s],
            device_id=sib, device_id_type=MESH)

    sums = [jnp.zeros((1, 1), F32), jnp.zeros((1, 1), F32)]
    for qi in (0, 2, 1, 3):
        l2, t = qi // 2, qi % 2
        off = offs[qi][4]
        if t == 0:
            piece = acc[c, l2, pl.ds(pl.multiple_of(off, 16), 48), :]
        else:
            x_copy(l2).wait_recv()
            piece = xrecv[l2]
        full = piece + diag[qi]
        slabs_v[slab(qi), pl.ds(pl.multiple_of(off, 16), 48), :] = full.astype(BF)
        for m in range(2):
            sums[m] = sums[m] + jnp.sum(full * subp[qi, m], keepdims=True)
        ag_copy(qi, 3).start()
        fw_copy(qi, 4).start()

    lane = iota((8, 128), 1)
    pvs[0] = jnp.where(lane == 0, sums[0], jnp.where(lane == 1, sums[1], F32(0)))
    hops = (*dims, sib, to_l, to_r)

    def pv_copy(n):
        return pltpu.make_async_remote_copy(
            src_ref=pvs.at[n], dst_ref=pvr.at[n], send_sem=pv_ss.at[n], recv_sem=pv_rs.at[n],
            device_id=hops[n], device_id_type=MESH)

    def pv_step(n):
        pv_copy(n).wait_recv()
        pvs[n + 1] = pvs[n] + pvr[n]

    for s in (3, 2, 1, 0):
        n = 3 - s
        pv_copy(n).start()
        for qi in (0, 2, 1, 3):
            rows = 384 >> s
            first = offs[qi][s] + (1 - bits[(qi + s) % 4]) * rows
            ref = slab_rows(slab(qi), first, rows)
            pltpu.make_async_remote_copy(
                src_ref=ref, dst_ref=ref, send_sem=ag_ss.at[qi, s], recv_sem=ag_rs.at[qi, s],
                device_id=dims[(qi + s) % 4], device_id_type=MESH).wait_recv()
            if s > 0:
                ag_copy(qi, s - 1).start()
            fw_copy(qi, s).start()
        pv_step(n)

    def o_copy(k):
        return pltpu.make_async_copy(slab_rows(k, 0, 768), out_hbm.at[k], out_sem.at[k])

    for t in range(2):
        for l2 in range(2):
            o_copy(t * 4 + c * 2 + l2).start()
    for n in (4, 5, 6):
        pv_copy(n).start()
        pv_step(n)
    proj_out[...] = pvs[7]
    for qi in range(4):
        for s in range(5):
            if s == 4:
                first, rows = offs[qi][4], 48
            else:
                rows = 384 >> s
                first = offs[qi][s] + (1 - bits[(qi + s) % 4]) * rows
            ref = slab_rows((qi % 2) * 4 + (1 - c) * 2 + qi // 2, first, rows)
            pltpu.make_async_remote_copy(
                src_ref=ref, dst_ref=ref, send_sem=fw_ss.at[qi, s], recv_sem=fw_rs.at[qi, s],
                device_id=sib, device_id_type=MESH).wait_recv()
    for t in range(2):
        for l2 in range(2):
            o_copy(t * 4 + (1 - c) * 2 + l2).start()
    for qi in range(4):
        d_copy(qi).wait_send()
        for s in range(4):
            rs_copy(qi, s).wait_send()
            ag_copy(qi, s).wait_send()
        for s in range(5):
            fw_copy(qi, s).wait_send()
    for l2 in range(2):
        x_copy(l2).wait_send()
    for n in range(7):
        pv_copy(n).wait_send()
    for k in range(8):
        o_copy(k).wait()


def compact_body(rstart, rsize, src, out, total):
    x = lax.axis_index("site")
    x_l = x + 1 - 2 * (x % 2)
    rows = src.shape[1]
    total[...] = jnp.zeros_like(total)

    def one(k, carry):
        xt = jnp.where(k // 4 == 0, x, x_l)
        half = (k // 2) % 2
        site = xt + half * (3 - 2 * xt)
        q = site * 4 + 2 * (k % 2)
        start = rstart[q]
        base = pl.multiple_of(jnp.minimum((start // 128) * 128, BOND - 512), 128)
        j = iota((384, 512), 0)
        odd = j >= W
        idx = jnp.where(odd, j - W, j)
        size = jnp.where(odd, rsize[q + 1], rsize[q])
        first = jnp.where(odd, rstart[q + 1], start) - base
        hot = one_hot((idx < size) & (iota((384, 512), 1) == idx + first))
        total[:, pl.ds(base, 512)] += jnp.dot(src[k], hot, preferred_element_type=F32)
        return carry

    lax.fori_loop(0, 8, one, 0)
    out[...] = total[...].astype(BF)


def sector_tables(sector_ids, sectors):
    labels = jnp.arange(sectors, dtype=jnp.int32)
    starts = jnp.sum((sector_ids[None, :] < labels[:, None]).astype(jnp.int32), axis=1)
    sizes = jnp.sum((sector_ids[None, :] == labels[:, None]).astype(jnp.int32), axis=1)
    return starts, sizes


def local(wavefunction, left_blocks, right_blocks, left_sector, right_sector, term_count,
          left_energy, right_energy, subspace):
    lstart, lsize = sector_tables(left_sector, 16)
    rstart, rsize = sector_tables(right_sector, 16)
    smem = pl.BlockSpec(memory_space=pltpu.SMEM)
    vmem = pl.BlockSpec(memory_space=pltpu.VMEM)
    hbm = pl.BlockSpec(memory_space=pl.ANY)
    dma = pltpu.SemaphoreType.DMA
    big = pltpu.CompilerParams(vmem_limit_bytes=67043328)
    pp, diag, subp = pl.pallas_call(
        prep_body,
        out_shape=(jax.ShapeDtypeStruct((8, 2048, 256), BF), jax.ShapeDtypeStruct((4, 48, 384), F32),
                   jax.ShapeDtypeStruct((4, 2, 48, 384), F32)),
        in_specs=[smem] * 4 + [vmem] * 3 + [hbm],
        out_specs=(hbm, vmem, vmem),
        scratch_shapes=[
            pltpu.VMEM((2048, BOND), BF),
            pltpu.VMEM((8, 2048, 256), BF),
            pltpu.VMEM((4, 160, BOND), BF),
            dma((4, 2)), dma((8,)),
        ],
        compiler_params=big,
        name="prepare",
    )(lstart, lsize, rstart, rsize, wavefunction,
      left_energy.reshape(1, BOND), right_energy.reshape(1, BOND), subspace)
    slabs, proj = pl.pallas_call(
        body,
        out_shape=(jax.ShapeDtypeStruct((8, 768, 384), BF), jax.ShapeDtypeStruct((8, 128), F32)),
        in_specs=[smem] * 2 + [hbm] * 3 + [vmem] * 2,
        out_specs=(hbm, vmem),
        scratch_shapes=[
            pltpu.VMEM((8, 768, 384), BF),
            pltpu.VMEM((8, 2048, 256), BF),
            pltpu.VMEM((2, 2, NS, 4, W, W), BF),
            pltpu.VMEM((NC, NS, 2, 3, W, 128), BF),
            pltpu.VMEM((NC, NS, 2, 3, W, 128), BF),
            pltpu.VMEM((NC, NS, 2, 3, 320, 128), BF),
            pltpu.VMEM((NC, NS, 2, 3, 320, 128), BF),
            pltpu.VMEM((768, NS * 256), BF),
            pltpu.VMEM((2, 2, 1536, 384), F32),
            pltpu.VMEM((2, 1536, 384), F32),
            pltpu.VMEM((4, 384, 384), F32),
            pltpu.VMEM((4, 192, 384), F32),
            pltpu.VMEM((4, 96, 384), F32),
            pltpu.VMEM((4, 48, 384), F32),
            pltpu.VMEM((2, 48, 384), F32),
            pltpu.VMEM((8, 8, 128), F32),
            pltpu.VMEM((7, 8, 128), F32),
            dma((2, 2)), dma, dma((8,)),
            dma((NC,)), dma((NC,)), dma((NC,)), dma((NC,)),
            dma((4,)), dma((4,)), dma((4, 4)), dma((4, 4)), dma((2,)), dma((2,)),
            dma((4, 4)), dma((4, 4)), dma((4, 5)), dma((4, 5)), dma((7,)), dma((7,)),
        ],
        compiler_params=pltpu.CompilerParams(
            collective_id=0, has_side_effects=True, vmem_limit_bytes=67043328),
        name="exchange",
    )(lsize, term_count, pp, left_blocks, right_blocks, diag, subp)
    rows = 192
    sigma = pl.pallas_call(
        compact_body,
        grid=(768 // rows,),
        out_shape=jax.ShapeDtypeStruct((768, BOND), BF),
        in_specs=[smem, smem, pl.BlockSpec((8, rows, 384), lambda i: (0, i, 0))],
        out_specs=pl.BlockSpec((rows, BOND), lambda i: (i, 0)),
        scratch_shapes=[pltpu.VMEM((rows, BOND), F32)],
        name="compact",
    )(rstart, rsize, slabs)
    return sigma.reshape(4, W, BOND), proj[0, :2]


def solution(mesh):
    in_specs = (P(), P("ops", "site", None, None), P("ops", "site", None, None), P(), P(), P("ops"),
                P(), P(), P(None, "site", None, None))
    out_specs = (P("site", None, None), P())
    return jax.shard_map(local, mesh=mesh, in_specs=in_specs, out_specs=out_specs, check_vma=False)
```

time: 728 us -> 172 us (0.24); the launches traced: 717 us -> 171 us
  waiting for transfers between devices: 347 us -> 0 us
  Pallas kernels: 0 us -> 167 us
  local copies, waits for them, and re-layouts: 122 us -> 1.18 us
  matrix products: 87 us -> 0 us
  loops' own time: 77.2 us -> 0 us
  other arithmetic: 53.9 us -> 1.48 us
  between operations: 21.6 us -> 1.29 us
  blocking collectives: 7.89 us -> 0 us
    psum x1 -> x0, waiting for transfers between devices: 282 us -> none  [local(): sigma_full = lax.psum(partial_value, 'ops') + diagonal]
    pallas_call x0 -> x3, Pallas kernels: none -> 167 us  [the longest x1 139 us: local(): pl.pallas_call(body, out_shape=(jax.ShapeDtypeStruct((8, 768, 384), BF),...]
    dot_general x60 -> x0, matrix products: 87 us -> none  [the longest x48 69.4 us: add_term(): lax.dot_general(window, one_block, (((1,), (1,)), ((), ())), preferred_el...]
    another operation x18 -> x0, loops' own time: 77.2 us -> none  [the longest x16 42.8 us: one_sector(): lax.fori_loop(0, active, add_term, jnp.zeros((row_count, widest), jnp.flo...]
    all_gather x1 -> x0, waiting for transfers between devices: 65 us -> none  [local(): part_blocks = lax.all_gather(right_blocks, 'site', axis=1, tiled=True)]
    dynamic_update_slice x16 -> x0, local copies, waits for them, and re-layouts: 47.4 us -> none  [one_sector(): lax.dynamic_update_slice_in_dim(summed, previous + added, col_start, 1)]
    dynamic_slice x35 -> x0, local copies, waits for them, and re-layouts: 24.8 us -> none  [the longest x16 9.42 us: one_sector(): keep_mask = block_mask(right_size[within], widest)]
    add x16 -> x0, other arithmetic: 18.4 us -> none  [one_sector(): previous + added]
  transfers between devices with their start and end apart: 2 -> 0, of which waited for: 2 -> 0; matrix products, arithmetic and copies ran while one was open for 7% -> 0% of each run, Pallas kernels for 0% -> 0%
where the time goes in v1:
time: 172 us; the launch traced here: 171 us
  Pallas kernels  167 us (97%)
    pallas_call x1, Pallas kernels, local(): pl.pallas_call(body, out_shape=(jax.ShapeDtypeStruct((8, 768, 384), BF),...  139 us
    pallas_call x1, Pallas kernels, local(): pl.pallas_call(prep_body, out_shape=(jax.ShapeDtypeStruct((8, 2048, 256),...  16 us
    pallas_call x1, Pallas kernels, local(): pl.pallas_call(compact_body, grid=(768 // rows,), out_shape=jax.ShapeDtyp...  12.9 us

profile of v1, /device:TPU:1, one launch (start us, length us, event | category | flops | bytes accessed | tf_op | source)
XLA Modules:
  0.0 171.5 jit_solution(9492011237864597249)
XLA Ops:
  1.3 1.5 convert_reduce_fusion
  2.8 16.0 %prepare.1 = (bf16[8,2048,256]{2,1,0:T(8,128)(2,1)}, f32[4,48,384]{2,1,0:T(8,128)}, f32[4,2,48,384]{3,2,1,0:T(8,128)}) custom-call(s32[16]{0:T(128)} %get-tuple-element.12.lstart, s32[16]{0:T(128)} %get-tuple-element.13.lsize, s32[16]{0:T(128)} %get-tuple-element.16.rstart, s32[16]{0:T(128)} %get-tuple-element.17.rsize, bf16[2048,2048]{1,0:T(8,128)(2,1)} %psi_v.1, ...), custom_call_target="tpu_custom_call" | custom-call | tf_op jit(solution)/shard_map/prepare/pallas_call | solution.py:506
  18.8 138.6 %exchange.1 = (bf16[8,768,384]{2,1,0:T(8,128)(2,1)}, f32[8,128]{1,0:T(8,128)}) custom-call(s32[16]{0:T(128)} %get-tuple-element.13.lsize, s32[1]{0:T(128)S(6)} %copy.11.count, bf16[8,2048,256]{2,1,0:T(8,128)(2,1)} %get-tuple-element.7.pp_hbm, bf16[8,4,192,192]{3,2,1,0:T(8,128)(2,1)} %left_hbm.1, bf16[8,4,192,192]{3,2,1,0:T(8,128)(2,1)} %right_hbm.1, ...), custom_call_target="tpu_custom_call" | custom-call | tf_op jit(solution)/shard_map/exchange/pallas_call | solution.py:522
  157.4 12.9 %compact.1 = bf16[768,2048]{1,0:T(8,128)(2,1)} custom-call(s32[16]{0:T(128)} %get-tuple-element.16.rstart, s32[16]{0:T(128)} %get-tuple-element.17.rsize, bf16[8,768,384]{2,1,0:T(8,128)(2,1)} %get-tuple-element.10.src), custom_call_target="tpu_custom_call" | custom-call | tf_op jit(solution)/shard_map/compact/pallas_call | solution.py:555
  170.3 1.2 slice_bitcast_fusion

commit v2 on v1

v2 whole, which is shorter than its diff:
```python
import jax
import jax.numpy as jnp
from jax import lax
from jax.experimental import pallas as pl
from jax.experimental.pallas import tpu as pltpu
from jax.sharding import PartitionSpec as P

W = 192
SLOTS = 8
NS = 2
NC = SLOTS // NS
BOND = 2048
BF = jnp.bfloat16
F32 = jnp.float32
MESH = pl.DeviceIdType.MESH


def iota(shape, dim):
    return lax.broadcasted_iota(jnp.int32, shape, dim)


def one_hot(mask):
    return jnp.where(mask, F32(1), F32(0)).astype(BF)


def packed_index(pos, parity):
    tail = pos - 64 * parity
    idx = jnp.where(pos < 128, pos, tail)
    ok = (pos < 128) | ((tail >= 128) & (tail < W))
    return idx, ok


CELLS = (
    ((0, ((0, 0), (0, 1))), (0, ((1, 0), (1, 1))), (0, ((0, 2), (1, 2))), (1, ((0, 0), (0, 1)))),
    ((0, ((0, 3), (1, 3))), (1, ((1, 0), (1, 1))), (1, ((0, 2), (1, 2))), (1, ((0, 3), (1, 3)))),
)
PLACE = {
    (h, l, r): (g, q, n)
    for g in range(2) for q, (h, pair) in enumerate(CELLS[g]) for n, (l, r) in enumerate(pair)
}
STEP = (192, 96, 48)


def piece_offsets(bits):
    offs = []
    for qi in range(4):
        off = [0]
        for s in range(3):
            off.append(off[-1] + bits[(qi + s) % 4] * STEP[s])
        offs.append(off)
    return offs


def cell_at(g, qi, n):
    (l0, r0), (l1, r1) = CELLS[g][qi][1]
    return l0 + n * (l1 - l0), r0 + n * (r1 - r0)


def label_bits(y, z):
    return (((y + 1) // 2) % 2, ((z + 1) // 2) % 2, y // 2, z // 2)


def prep_body(
    lstart, lsize, rstart, rsize, psi_v, lenergy, renergy, sub_hbm,
    pp_hbm, diag, subp, gath, pp, stack, sub_sem, pp_sem,
):
    x = lax.axis_index("site")
    o = lax.axis_index("ops")
    c = o % 2
    x_l = x + 1 - 2 * (x % 2)
    x_r = 3 - x
    offs = piece_offsets(label_bits((o // 2) % 4, o // 8))

    def piece(g, qi):
        off = offs[qi][3]
        n = off // W
        l, r = cell_at(g, qi, n)
        return 2 * l + c, off - n * W, r

    def sub_copy(g, qi, k):
        i, a0, r = piece(g, qi)
        return pltpu.make_async_copy(
            sub_hbm.at[k, i, pl.ds(pl.multiple_of(a0, 16), 48), :],
            stack.at[g * 4 + qi, pl.ds(48 + 48 * k, 48), :], sub_sem.at[g * 4 + qi, k])

    for g in range(2):
        for qi in range(4):
            for k in range(2):
                sub_copy(g, qi, k).start()

    def row_hot(q, first, rows, packed):
        rs = lstart[q]
        base = pl.multiple_of(jnp.minimum((rs // 16) * 16, BOND - 256), 16)
        pos = iota((rows, 256), 0) + first
        if packed:
            idx, ok = packed_index(pos, q % 2)
        else:
            idx, ok = pos, pos < W
        ok = ok & (idx < lsize[q])
        return base, one_hot(ok & (iota((rows, 256), 1) == idx + (rs - base)))

    def rows_of(i, carry):
        q = jnp.where(i < 4, x * 4 + i, x_l * 4 + i - 4)
        base, hot = row_hot(q, 0, 256, True)
        for n in range(4):
            win = psi_v[pl.ds(base, 256), pl.ds(n * 512, 512)]
            gath[pl.ds(pl.multiple_of(i * 256, 256), 256), pl.ds(n * 512, 512)] = jnp.dot(
                hot, win, preferred_element_type=F32).astype(BF)
        return carry

    lax.fori_loop(0, 8, rows_of, 0)

    def pp_copy(j):
        return pltpu.make_async_copy(pp.at[j], pp_hbm.at[j], pp_sem.at[j])

    def cols_of(j, carry):
        q = jnp.where(j < 4, x * 4 + j, x_r * 4 + j - 4)
        cs = rstart[q]
        cb = pl.multiple_of(jnp.minimum((cs // 128) * 128, BOND - 384), 128)
        idx, ok = packed_index(iota((384, 256), 1), q % 2)
        ok = ok & (idx < rsize[q])
        hot = one_hot(ok & (iota((384, 256), 0) == idx + (cs - cb)))
        for m in range(4):
            win = gath[pl.ds(m * 512, 512), pl.ds(cb, 384)]
            pp[j, pl.ds(m * 512, 512), :] = jnp.dot(win, hot, preferred_element_type=F32).astype(BF)
        pp_copy(j).start()
        return carry

    lax.fori_loop(0, 8, cols_of, 0)

    re = renergy[...]
    hi = re.astype(BF)
    rem = re - hi.astype(F32)
    mid = rem.astype(BF)
    low = (rem - mid.astype(F32)).astype(BF)
    rows16 = iota((16, BOND), 0)
    er3 = jnp.where(rows16 == 0, hi.astype(F32),
                    jnp.where(rows16 == 1, mid.astype(F32),
                              jnp.where(rows16 == 2, low.astype(F32), F32(0)))).astype(BF)
    for g in range(2):
        for qi in range(4):
            at = g * 4 + qi
            i, a0, r = piece(g, qi)
            q = x * 4 + i
            base, hot = row_hot(q, a0, 48, False)
            for n in range(4):
                win = psi_v[pl.ds(base, 256), pl.ds(n * 512, 512)]
                stack[at, pl.ds(0, 48), pl.ds(n * 512, 512)] = jnp.dot(
                    hot, win, preferred_element_type=F32).astype(BF)
            stack[at, pl.ds(144, 16), :] = er3
            for k in range(2):
                sub_copy(g, qi, k).wait()
            xt = x if CELLS[g][qi][0] == 0 else x_l
            site = xt + (r // 2) * (3 - 2 * xt)
            total = None
            for par in range(2):
                qr = site * 4 + 2 * (r % 2) + par
                cs = rstart[qr]
                cb = pl.multiple_of(jnp.minimum((cs // 128) * 128, BOND - 384), 128)
                j = iota((384, 384), 1) - W * par
                hot2 = one_hot((j >= 0) & (j < W) & (j < rsize[qr]) & (iota((384, 384), 0) == j + (cs - cb)))
                part = jnp.dot(stack[at, :, pl.ds(cb, 384)], hot2, preferred_element_type=F32)
                total = part if total is None else total + part
            lb = pl.multiple_of(jnp.minimum((lstart[q] // 128) * 128, BOND - 384), 128)
            shift = lstart[q] - lb + a0
            pick = iota((48, 384), 1) == iota((48, 384), 0) + shift
            el = jnp.sum(jnp.where(pick, lenergy[:, pl.ds(lb, 384)], F32(0)), axis=1, keepdims=True)
            er = total[144:145] + total[145:146] + total[146:147]
            diag[at] = (el + er) * total[:48]
            subp[at, 0] = total[48:96]
            subp[at, 1] = total[96:144]

    for j in range(8):
        pp_copy(j).wait()


def body(
    lsize, count, pp_hbm, left_hbm, right_hbm, diag, subp,
    out_hbm, proj_out,
    slabs, pp, raw, lown, lfor, rown, rfor, li, acc,
    drecv, rs0, rs1, rs2, rs3, xrecv, pvs, pvr,
    raw_sem, pp_sem, out_sem,
    l_ss, l_rs, r_ss, r_rs, d_ss, d_rs, rs_ss, rs_rs, x_ss, x_rs,
    ag_ss, ag_rs, fw_ss, fw_rs, pv_ss, pv_rs,
):
    x = lax.axis_index("site")
    o = lax.axis_index("ops")
    c = o % 2
    y = (o // 2) % 4
    z = o // 8
    x_l = x + 1 - 2 * (x % 2)
    x_r = 3 - x
    to_l = {"site": x_l}
    to_r = {"site": x_r}
    sib = {"ops": o + 1 - 2 * c}
    y_a = y + 1 - 2 * (y % 2)
    z_a = z + 1 - 2 * (z % 2)
    y_c = 3 - y_a
    z_c = 3 - z_a
    x_c = 3 - x_l
    dims = (
        {"ops": o + 2 * (y_a - y)},
        {"ops": o + 8 * (z_a - z)},
        {"ops": o + 2 * (3 - 2 * y)},
        {"ops": o + 8 * (3 - 2 * z)},
    )
    far = ({"ops": o + 2 * (y_c - y)}, {"ops": o + 8 * (z_c - z)}, {"site": x_c})
    bits = label_bits(y, z)
    offs = piece_offsets(bits)

    def raw_copies(m):
        buf = m % 2
        return (
            pltpu.make_async_copy(left_hbm.at[pl.ds(NS * m, NS)], raw.at[buf, 0], raw_sem.at[buf, 0]),
            pltpu.make_async_copy(right_hbm.at[pl.ds(NS * m, NS)], raw.at[buf, 1], raw_sem.at[buf, 1]),
        )

    for m in range(2):
        for cp in raw_copies(m):
            cp.start()
    pp_copy = pltpu.make_async_copy(pp_hbm, pp, pp_sem)
    pp_copy.start()

    pvr[...] = jnp.zeros_like(pvr)
    barrier = pltpu.get_barrier_semaphore()
    for who in (to_l, to_r, sib, *dims, *far):
        pl.semaphore_signal(barrier, inc=1, device_id=who, device_id_type=MESH)

    zrow = jnp.zeros((2, SLOTS, 3, 64, 128), BF)
    for buf in (rown, rfor):
        for start in (0, 256):
            buf[:, :, :, pl.ds(start, 64), :] = zrow

    def l_copy(p, m):
        at = pl.ds(NS * m, NS)
        return pltpu.make_async_remote_copy(
            src_ref=lown.at[p, at], dst_ref=lfor.at[p, at], send_sem=l_ss.at[p, m], recv_sem=l_rs.at[p, m],
            device_id=to_l, device_id_type=MESH)

    def r_copy(p, m):
        at = pl.ds(NS * m, NS)
        rows = pl.ds(64, W)
        return pltpu.make_async_remote_copy(
            src_ref=rown.at[p, at, :, rows, :], dst_ref=rfor.at[p, at, :, rows, :],
            send_sem=r_ss.at[p, m], recv_sem=r_rs.at[p, m], device_id=to_r, device_id_type=MESH)

    def pack(m):
        buf = m % 2

        def one(k, carry):
            s = k // 2
            p = k % 2
            slot = NS * m + s
            row = iota((W, 128), 0)
            live = slot < count[0]
            keep = []
            for par in range(2):
                size = jnp.where(live, lsize[x * 4 + 2 * p + par], 0)
                keep.append(one_hot(row < size))
            ev = raw[buf, 0, s, 2 * p]
            od = raw[buf, 0, s, 2 * p + 1]
            lown[p, slot, 0] = ev[:, :128] * keep[0]
            lown[p, slot, 1] = od[:, :128] * keep[1]
            lown[p, slot, 2] = jnp.concatenate(
                [ev[:, 128:] * keep[0][:, :64], od[:, 128:] * keep[1][:, :64]], axis=1)
            ev = raw[buf, 1, s, 2 * p]
            od = raw[buf, 1, s, 2 * p + 1]
            rows = pl.ds(64, W)
            rown[p, slot, 0, rows, :] = ev[:, :128]
            rown[p, slot, 1, rows, :] = od[:, :128]
            rown[p, slot, 2, rows, :] = jnp.concatenate([ev[:, 128:], od[:, 128:]], axis=1)
            return carry

        lax.fori_loop(0, 2 * NS, one, 0)

    for m in range(NC):
        for cp in raw_copies(m):
            cp.wait()
        pack(m)
        if m == 0:
            pl.semaphore_wait(barrier, 10)
        if m + 2 < NC:
            for cp in raw_copies(m + 2):
                cp.start()
        l_copy(0, m).start()
        r_copy(0, m).start()
    for m in range(NC):
        l_copy(1, m).start()
        r_copy(1, m).start()

    def clear(k, carry):
        for g in range(2):
            for q in range(4):
                acc[g, q, k // 2, pl.ds(pl.multiple_of((k % 2) * W, W), W), :] = jnp.zeros((W, 384), F32)
        return carry

    lax.fori_loop(0, 4, clear, 0)
    pp_copy.wait()

    def product(m, r, lefts):
        rsrc = rown if r < 2 else rfor
        slots = pl.ds(NS * m, NS)
        for par in range(2):
            j = 2 * r + par
            for n, (h, l) in enumerate(lefts):
                lsrc = lown if h == 0 else lfor
                tail = lsrc[l, slots, 2].reshape(NS * W, 128)
                for pa in range(2):
                    lhs = jnp.concatenate([lsrc[l, slots, pa].reshape(NS * W, 128), tail], axis=1)
                    img = jnp.dot(lhs, pp[j, pl.ds((h * 4 + 2 * l + pa) * 256, 256), :],
                                  preferred_element_type=F32).astype(BF)
                    for s in range(NS):
                        li[pl.ds((2 * n + pa) * W, W), pl.ds(s * 256, 256)] = img[s * W:(s + 1) * W]
            rows = pl.ds(64 - 64 * par, 256)
            rhs = jnp.concatenate(
                [rsrc[r % 2, NS * m + s, k, rows, :] for s in range(NS) for k in (par, 2)], axis=1)
            lanes = pl.ds(128 * par, 256)
            for n, (h, l) in enumerate(lefts):
                g, q, cell = PLACE[(h, l, r)]
                res = lax.dot_general(li[pl.ds(2 * n * W, 2 * W), :], rhs, (((1,), (1,)), ((), ())),
                                      preferred_element_type=F32)
                for pa in range(2):
                    acc[g, q, pa, pl.ds(cell * W, W), lanes] += res[pa * W:(pa + 1) * W]

    def arrive(p, m):
        l_copy(p, m).wait()
        r_copy(p, m).wait()

    def d_copy(g, qi):
        return pltpu.make_async_remote_copy(
            src_ref=acc.at[g, qi, 1 - c], dst_ref=drecv.at[g, qi],
            send_sem=d_ss.at[g, qi], recv_sem=d_rs.at[g, qi], device_id=sib, device_id_type=MESH)

    rsb = (rs0, rs1, rs2, rs3)

    def rs_copy(g, qi, s):
        d = (qi + s) % 4
        if s < 3:
            rows = STEP[s]
            first = offs[qi][s] + (1 - bits[d]) * rows
        else:
            rows, first = 48, offs[qi][3]
        return pltpu.make_async_remote_copy(
            src_ref=acc.at[g, qi, c, pl.ds(pl.multiple_of(first, 16), rows), :],
            dst_ref=rsb[s].at[g, qi], send_sem=rs_ss.at[g, qi, s], recv_sem=rs_rs.at[g, qi, s],
            device_id=dims[d], device_id_type=MESH)

    def add_rows(g, qi, first, src, src_first, rows):
        def step(k, carry):
            at = pl.ds(pl.multiple_of(first + k * 48, 16), 48)
            acc[g, qi, c, at, :] += src[pl.ds(pl.multiple_of(src_first + k * 48, 16), 48), :]
            return carry

        lax.fori_loop(0, rows // 48, step, 0)

    def core_sum(g):
        for qi in range(4):
            d_copy(g, qi).wait_recv()
            there = (1 - bits[qi]) * 192
            here = bits[qi] * 192
            add_rows(g, qi, there, drecv.at[g, qi], there, 192)
            rs_copy(g, qi, 0).start()
            add_rows(g, qi, here, drecv.at[g, qi], here, 192)

    def x_copy(g, qi):
        return pltpu.make_async_remote_copy(
            src_ref=acc.at[g, qi, c, pl.ds(pl.multiple_of(offs[qi][3], 16), 48), :], dst_ref=xrecv.at[g, qi],
            send_sem=x_ss.at[g, qi], recv_sem=x_rs.at[g, qi], device_id=to_l, device_id_type=MESH)

    def reduce_step(g, s):
        for qi in range(4):
            rs_copy(g, qi, s).wait_recv()
            if s == 3:
                rs_copy(g, qi, 3).wait_send()
                add_rows(g, qi, offs[qi][3], rs3.at[g, qi], 0, 48)
                if CELLS[g][qi][0] == 1:
                    x_copy(g, qi).start()
            else:
                add_rows(g, qi, offs[qi][s + 1], rsb[s].at[g, qi], 0, STEP[s])
                rs_copy(g, qi, s + 1).start()

    def rows_at(g, qi, first, rows, core):
        n = first // W
        l, r = cell_at(g, qi, n)
        at = (2 * l + core) * W + first - n * W
        return CELLS[g][qi][0] * 4 + r, pl.ds(pl.multiple_of(at, 16), rows)

    def ag_copy(g, qi, s, mine):
        d = (qi + s) % 4
        first = offs[qi][s + 1] if mine else offs[qi][s] + (1 - bits[d]) * STEP[s]
        k, at = rows_at(g, qi, first, STEP[s], c)
        return pltpu.make_async_remote_copy(
            src_ref=slabs.at[k, at, :], dst_ref=slabs.at[k, at, :],
            send_sem=ag_ss.at[g, qi, s], recv_sem=ag_rs.at[g, qi, s],
            device_id=dims[d], device_id_type=MESH)

    def fw_copy(g, qi, s, core):
        if s == 3:
            first, rows = offs[qi][3], 48
        else:
            first, rows = offs[qi][s] + (1 - bits[(qi + s) % 4]) * STEP[s], STEP[s]
        k, at = rows_at(g, qi, first, rows, core)
        return pltpu.make_async_remote_copy(
            src_ref=slabs.at[k, at, :], dst_ref=slabs.at[k, at, :],
            send_sem=fw_ss.at[g, qi, s], recv_sem=fw_rs.at[g, qi, s],
            device_id=sib, device_id_type=MESH)

    sums = [jnp.zeros((1, 1), F32), jnp.zeros((1, 1), F32)]

    def finish(g, h):
        for qi in range(4):
            if CELLS[g][qi][0] != h:
                continue
            off = offs[qi][3]
            if h == 0:
                part = acc[g, qi, c, pl.ds(pl.multiple_of(off, 16), 48), :]
            else:
                x_copy(g, qi).wait_recv()
                part = xrecv[g, qi]
            full = part + diag[g * 4 + qi]
            k, at = rows_at(g, qi, off, 48, c)
            slabs[k, at, :] = full.astype(BF)
            ag_copy(g, qi, 2, True).start()
            fw_copy(g, qi, 3, c).start()
            weight = (1 - bits[(qi + 3) % 4]).astype(F32)
            for k in range(2):
                sums[k] = sums[k] + weight * jnp.sum(full * subp[g * 4 + qi, k], keepdims=True)

    def gather_step(g, s, h=None):
        for qi in range(4):
            if h is not None and CELLS[g][qi][0] != h:
                continue
            ag_copy(g, qi, s, False).wait_recv()
            if s > 0:
                ag_copy(g, qi, s - 1, True).start()
            fw_copy(g, qi, s, c).start()

    def step0(m, carry):
        for r in range(2):
            product(m, r, ((0, 0), (0, 1)))
        return carry

    lax.fori_loop(0, NC, step0, 0)

    def step1(m, carry):
        arrive(0, m)
        for r in range(2):
            product(m, r, ((1, 0),))
        product(m, 2, ((0, 0), (0, 1), (1, 0)))
        return carry

    lax.fori_loop(0, NC, step1, 0)
    for qi in range(4):
        d_copy(0, qi).start()

    def first_half(m):
        arrive(1, m)
        for r in range(3):
            product(m, r, ((1, 1),))

    def second_half(m):
        product(m, 3, ((0, 0), (0, 1), (1, 0), (1, 1)))

    first_half(0)
    core_sum(0)
    second_half(0)
    first_half(1)
    reduce_step(0, 0)
    second_half(1)
    reduce_step(0, 1)
    first_half(2)
    reduce_step(0, 2)
    second_half(2)
    reduce_step(0, 3)
    finish(0, 0)
    first_half(3)
    for qi in (1, 2):
        d_copy(1, qi).start()
    second_half(3)
    for qi in (0, 3):
        d_copy(1, qi).start()
    finish(0, 1)
    gather_step(0, 2)
    core_sum(1)
    gather_step(0, 1)
    reduce_step(1, 0)
    gather_step(0, 0)
    reduce_step(1, 1)
    reduce_step(1, 2)
    reduce_step(1, 3)
    finish(1, 0)
    finish(1, 1)

    lane = iota((8, 128), 1)
    pvs[0] = jnp.where(lane == 0, sums[0], jnp.where(lane == 1, sums[1], F32(0)))
    rounds = (
        (c, ((sib, 1 - c),)),
        (y, ((dims[0], y_a), (dims[2], 3 - y), (far[0], y_c))),
        (z, ((dims[1], z_a), (dims[3], 3 - z), (far[1], z_c))),
        (x, ((to_l, x_l), (to_r, x_r), (far[2], x_c))),
    )

    def pv_copy(n, i, slot):
        return pltpu.make_async_remote_copy(
            src_ref=pvs.at[n], dst_ref=pvr.at[n, slot], send_sem=pv_ss.at[n, i], recv_sem=pv_rs.at[n, slot],
            device_id=rounds[n][1][i][0], device_id_type=MESH)

    def pv_send(n):
        me, others = rounds[n]
        for i in range(len(others)):
            pv_copy(n, i, me).start()
        pvr[n, me] = pvs[n]

    def pv_sum(n):
        me, others = rounds[n]
        for i, (who, slot) in enumerate(others):
            pv_copy(n, i, slot).wait_recv()
        pvs[n + 1] = (pvr[n, 0] + pvr[n, 1]) + (pvr[n, 2] + pvr[n, 3])

    def o_copy(k, core):
        rows = tuple(pl.ds((2 * l + core) * W, W) for l in range(2))
        return [pltpu.make_async_copy(slabs.at[k, at, :], out_hbm.at[k, at, :], out_sem.at[k, core, l])
                for l, at in enumerate(rows)]

    pv_send(0)
    for n, s in enumerate((2, 1, 0)):
        gather_step(1, s)
        pv_sum(n)
        pv_send(n + 1)
    for k in range(8):
        for cp in o_copy(k, c):
            cp.start()
    for g in range(2):
        for s in (3, 2, 1, 0):
            for qi in range(4):
                fw_copy(g, qi, s, 1 - c).wait_recv()
    for k in range(8):
        for cp in o_copy(k, 1 - c):
            cp.start()
    pv_sum(3)
    proj_out[...] = pvs[4]
    for g in range(2):
        for qi in range(4):
            d_copy(g, qi).wait_send()
            for s in range(3):
                rs_copy(g, qi, s).wait_send()
                ag_copy(g, qi, s, True).wait_send()
            for s in range(4):
                fw_copy(g, qi, s, c).wait_send()
            if CELLS[g][qi][0] == 1:
                x_copy(g, qi).wait_send()
    for n in range(4):
        for i in range(len(rounds[n][1])):
            pv_copy(n, i, rounds[n][0]).wait_send()
    for k in range(8):
        for core in (c, 1 - c):
            for cp in o_copy(k, core):
                cp.wait()


def compact_body(rstart, rsize, src, out):
    x = lax.axis_index("site")
    k = pl.program_id(0)
    x_l = x + 1 - 2 * (x % 2)

    @pl.when(k == 0)
    def _():
        out[...] = jnp.zeros_like(out)

    xt = jnp.where(k // 4 == 0, x, x_l)
    site = xt + ((k // 2) % 2) * (3 - 2 * xt)
    q = site * 4 + 2 * (k % 2)
    start = rstart[q]
    base = pl.multiple_of(jnp.minimum((start // 128) * 128, BOND - 512), 128)
    j = iota((384, 512), 0)
    odd = j >= W
    idx = jnp.where(odd, j - W, j)
    size = jnp.where(odd, rsize[q + 1], rsize[q])
    first = jnp.where(odd, rstart[q + 1], start) - base
    hot = one_hot((idx < size) & (iota((384, 512), 1) == idx + first))
    out[:, pl.ds(base, 512)] += jnp.dot(src[0], hot, preferred_element_type=F32).astype(BF)


def sector_tables(sector_ids, sectors):
    labels = jnp.arange(sectors, dtype=jnp.int32)
    starts = jnp.sum((sector_ids[None, :] < labels[:, None]).astype(jnp.int32), axis=1)
    sizes = jnp.sum((sector_ids[None, :] == labels[:, None]).astype(jnp.int32), axis=1)
    return starts, sizes


def local(wavefunction, left_blocks, right_blocks, left_sector, right_sector, term_count,
          left_energy, right_energy, subspace):
    lstart, lsize = sector_tables(left_sector, 16)
    rstart, rsize = sector_tables(right_sector, 16)
    smem = pl.BlockSpec(memory_space=pltpu.SMEM)
    vmem = pl.BlockSpec(memory_space=pltpu.VMEM)
    hbm = pl.BlockSpec(memory_space=pl.ANY)
    dma = pltpu.SemaphoreType.DMA
    big = pltpu.CompilerParams(vmem_limit_bytes=67043328)
    pp, diag, subp = pl.pallas_call(
        prep_body,
        out_shape=(jax.ShapeDtypeStruct((8, 2048, 256), BF), jax.ShapeDtypeStruct((8, 48, 384), F32),
                   jax.ShapeDtypeStruct((8, 2, 48, 384), F32)),
        in_specs=[smem] * 4 + [vmem] * 3 + [hbm],
        out_specs=(hbm, vmem, vmem),
        scratch_shapes=[
            pltpu.VMEM((2048, BOND), BF),
            pltpu.VMEM((8, 2048, 256), BF),
            pltpu.VMEM((8, 160, BOND), BF),
            dma((8, 2)), dma((8,)),
        ],
        compiler_params=big,
        name="prepare",
    )(lstart, lsize, rstart, rsize, wavefunction,
      left_energy.reshape(1, BOND), right_energy.reshape(1, BOND), subspace)
    slabs, proj = pl.pallas_call(
        body,
        out_shape=(jax.ShapeDtypeStruct((8, 768, 384), BF), jax.ShapeDtypeStruct((8, 128), F32)),
        in_specs=[smem] * 2 + [hbm] * 3 + [vmem] * 2,
        out_specs=(hbm, vmem),
        scratch_shapes=[
            pltpu.VMEM((8, 768, 384), BF),
            pltpu.VMEM((8, 2048, 256), BF),
            pltpu.VMEM((2, 2, NS, 4, W, W), BF),
            pltpu.VMEM((2, SLOTS, 3, W, 128), BF),
            pltpu.VMEM((2, SLOTS, 3, W, 128), BF),
            pltpu.VMEM((2, SLOTS, 3, 320, 128), BF),
            pltpu.VMEM((2, SLOTS, 3, 320, 128), BF),
            pltpu.VMEM((1536, NS * 256), BF),
            pltpu.VMEM((2, 4, 2, 384, 384), F32),
            pltpu.VMEM((2, 4, 384, 384), F32),
            pltpu.VMEM((2, 4, 192, 384), F32),
            pltpu.VMEM((2, 4, 96, 384), F32),
            pltpu.VMEM((2, 4, 48, 384), F32),
            pltpu.VMEM((2, 4, 48, 384), F32),
            pltpu.VMEM((2, 4, 48, 384), F32),
            pltpu.VMEM((5, 8, 128), F32),
            pltpu.VMEM((4, 4, 8, 128), F32),
            dma((2, 2)), dma, dma((8, 2, 2)),
            dma((2, NC)), dma((2, NC)), dma((2, NC)), dma((2, NC)),
            dma((2, 4)), dma((2, 4)), dma((2, 4, 4)), dma((2, 4, 4)), dma((2, 4)), dma((2, 4)),
            dma((2, 4, 3)), dma((2, 4, 3)), dma((2, 4, 4)), dma((2, 4, 4)), dma((4, 3)), dma((4, 4)),
        ],
        compiler_params=pltpu.CompilerParams(
            collective_id=0, has_side_effects=True, vmem_limit_bytes=67043328),
        name="exchange",
    )(lsize, term_count, pp, left_blocks, right_blocks, diag, subp)
    sigma = pl.pallas_call(
        compact_body,
        grid=(8,),
        out_shape=jax.ShapeDtypeStruct((768, BOND), BF),
        in_specs=[smem, smem, pl.BlockSpec((1, 768, 384), lambda k: (k, 0, 0))],
        out_specs=pl.BlockSpec((768, BOND), lambda k: (0, 0)),
        name="compact",
    )(rstart, rsize, slabs)
    return sigma.reshape(4, W, BOND), proj[0, :2]


def solution(mesh):
    in_specs = (P(), P("ops", "site", None, None), P("ops", "site", None, None), P(), P(), P("ops"),
                P(), P(), P(None, "site", None, None))
    out_specs = (P("site", None, None), P())
    return jax.shard_map(local, mesh=mesh, in_specs=in_specs, out_specs=out_specs, check_vma=False)
```

time: 172 us -> 150 us (0.87)
  Pallas kernels: 167 us -> 144 us
    pallas_call x1, Pallas kernels: 139 us -> 117 us  [local(): pl.pallas_call(body, out_shape=(jax.ShapeDtypeStruct((8, 768, 384), BF),...]
    pallas_call x1, Pallas kernels: 12.9 us -> 9.5 us  [local(): pl.pallas_call(compact_body, grid=(8,), out_shape=jax.ShapeDtypeStruct((7...]
    pallas_call x1, Pallas kernels: 16 us -> 18.3 us  [local(): pl.pallas_call(prep_body, out_shape=(jax.ShapeDtypeStruct((8, 2048, 256),...]
where the time goes in v2:
time: 150 us; the launch traced here: 148 us
  Pallas kernels  144 us (96%)
  other arithmetic  1.5 us (1%)
    pallas_call x1, Pallas kernels, local(): pl.pallas_call(body, out_shape=(jax.ShapeDtypeStruct((8, 768, 384), BF),...  117 us
    pallas_call x1, Pallas kernels, local(): pl.pallas_call(prep_body, out_shape=(jax.ShapeDtypeStruct((8, 2048, 256),...  18.3 us
    pallas_call x1, Pallas kernels, local(): pl.pallas_call(compact_body, grid=(8,), out_shape=jax.ShapeDtypeStruct((7...  9.5 us

profile of v2, /device:TPU:1, one launch (start us, length us, event | category | flops | bytes accessed | tf_op | source)
XLA Modules:
  0.0 148.4 jit_solution(6423977188854600353)
XLA Ops:
  1.3 1.5 %convert_reduce_fusion = (s32[16]{0:T(128)}, s32[16]{0:T(128)}, s32[16]{0:T(128)}, s32[16]{0:T(128)}) fusion(s32[2048]{0:T(1024)} %param.12, s32[2048]{0:T(1024)} %param.13), kind=kLoop, calls=%fused_computation | loop fusion | flops 393152 | bytes 16640 | tf_op jit(solution)/shard_map/reduce_sum | solution.py:586
  2.8 18.3 %prepare.1 = (bf16[8,2048,256]{2,1,0:T(8,128)(2,1)}, f32[8,48,384]{2,1,0:T(8,128)}, f32[8,2,48,384]{3,2,1,0:T(8,128)}) custom-call(s32[16]{0:T(128)} %get-tuple-element.12.lstart, s32[16]{0:T(128)} %get-tuple-element.13.lsize, s32[16]{0:T(128)} %get-tuple-element.16.rstart, s32[16]{0:T(128)} %get-tuple-element.17.rsize, bf16[2048,2048]{1,0:T(8,128)(2,1)} %psi_v.1, ...), custom_call_target="tpu_custom_call" | custom-call | tf_op jit(solution)/shard_map/prepare/pallas_call | solution.py:600
  21.0 116.7 %exchange.1 = (bf16[8,768,384]{2,1,0:T(8,128)(2,1)}, f32[8,128]{1,0:T(8,128)}) custom-call(s32[16]{0:T(128)} %get-tuple-element.13.lsize, s32[1]{0:T(128)S(6)} %copy.11.count, bf16[8,2048,256]{2,1,0:T(8,128)(2,1)} %get-tuple-element.7.pp_hbm, bf16[8,4,192,192]{3,2,1,0:T(8,128)(2,1)} %left_hbm.1, bf16[8,4,192,192]{3,2,1,0:T(8,128)(2,1)} %right_hbm.1, ...), custom_call_target="tpu_custom_call" | custom-call | tf_op jit(solution)/shard_map/exchange/pallas_call | solution.py:616
  137.7 9.5 %compact.1 = bf16[768,2048]{1,0:T(8,128)(2,1)} custom-call(s32[16]{0:T(128)} %get-tuple-element.16.rstart, s32[16]{0:T(128)} %get-tuple-element.17.rsize, bf16[8,768,384]{2,1,0:T(8,128)(2,1)} %get-tuple-element.10.src), custom_call_target="tpu_custom_call" | custom-call | tf_op jit(solution)/shard_map/compact/pallas_call | solution.py:648
  147.2 1.2 slice_bitcast_fusion

commit v3 on v2

--- a/solution.py
+++ b/solution.py
@@ -417,7 +417,7 @@
             else:
                 x_copy(g, qi).wait_recv()
                 part = xrecv[g, qi]
-            full = part + diag[g * 4 + qi]
+            full = part + diag[g * 4 + qi + jnp.minimum(lsize[0], 0)]
             k, at = rows_at(g, qi, off, 48, c)
             slabs[k, at, :] = full.astype(BF)
             ag_copy(g, qi, 2, True).start()

time: 150 us -> 150 us (level)
  no operation moved by 1% of the time
where the time goes in v3:
time: 150 us; the launch traced here: 148 us
  Pallas kernels  144 us (96%)
  other arithmetic  1.5 us (1%)
    pallas_call x1, Pallas kernels, local(): pl.pallas_call(body, out_shape=(jax.ShapeDtypeStruct((8, 768, 384), BF),...  117 us
    pallas_call x1, Pallas kernels, local(): pl.pallas_call(prep_body, out_shape=(jax.ShapeDtypeStruct((8, 2048, 256),...  18.3 us
    pallas_call x1, Pallas kernels, local(): pl.pallas_call(compact_body, grid=(8,), out_shape=jax.ShapeDtypeStruct((7...  9.5 us

profile of v3, /device:TPU:1, one launch (start us, length us, event | category | flops | bytes accessed | tf_op | source)
XLA Modules:
  0.0 148.4 jit_solution(8684992536414486295)
XLA Ops:
  1.3 1.5 %convert_reduce_fusion = (s32[16]{0:T(128)}, s32[16]{0:T(128)}, s32[16]{0:T(128)}, s32[16]{0:T(128)}) fusion(s32[2048]{0:T(1024)} %param.12, s32[2048]{0:T(1024)} %param.13), kind=kLoop, calls=%fused_computation | loop fusion | flops 393152 | bytes 16640 | tf_op jit(solution)/shard_map/reduce_sum | solution.py:586
  2.8 18.3 %prepare.1 = (bf16[8,2048,256]{2,1,0:T(8,128)(2,1)}, f32[8,48,384]{2,1,0:T(8,128)}, f32[8,2,48,384]{3,2,1,0:T(8,128)}) custom-call(s32[16]{0:T(128)} %get-tuple-element.12.lstart, s32[16]{0:T(128)} %get-tuple-element.13.lsize, s32[16]{0:T(128)} %get-tuple-element.16.rstart, s32[16]{0:T(128)} %get-tuple-element.17.rsize, bf16[2048,2048]{1,0:T(8,128)(2,1)} %psi_v.1, ...), custom_call_target="tpu_custom_call" | custom-call | tf_op jit(solution)/shard_map/prepare/pallas_call | solution.py:600
  21.1 116.7 %exchange.1 = (bf16[8,768,384]{2,1,0:T(8,128)(2,1)}, f32[8,128]{1,0:T(8,128)}) custom-call(s32[16]{0:T(128)} %get-tuple-element.13.lsize, s32[1]{0:T(128)S(6)} %copy.11.count, bf16[8,2048,256]{2,1,0:T(8,128)(2,1)} %get-tuple-element.7.pp_hbm, bf16[8,4,192,192]{3,2,1,0:T(8,128)(2,1)} %left_hbm.1, bf16[8,4,192,192]{3,2,1,0:T(8,128)(2,1)} %right_hbm.1, ...), custom_call_target="tpu_custom_call" | custom-call | tf_op jit(solution)/shard_map/exchange/pallas_call | solution.py:616
  137.7 9.5 %compact.1 = bf16[768,2048]{1,0:T(8,128)(2,1)} custom-call(s32[16]{0:T(128)} %get-tuple-element.16.rstart, s32[16]{0:T(128)} %get-tuple-element.17.rsize, bf16[8,768,384]{2,1,0:T(8,128)(2,1)} %get-tuple-element.10.src), custom_call_target="tpu_custom_call" | custom-call | tf_op jit(solution)/shard_map/compact/pallas_call | solution.py:648
  147.2 1.2 slice_bitcast_fusion

commit v4 on v2

v4 whole, which is shorter than its diff:
```python
import jax
import jax.numpy as jnp
from jax import lax
from jax.experimental import pallas as pl
from jax.experimental.pallas import tpu as pltpu
from jax.sharding import PartitionSpec as P

W = 192
SLOTS = 8
NS = 2
NC = SLOTS // NS
BOND = 2048
BF = jnp.bfloat16
F32 = jnp.float32
MESH = pl.DeviceIdType.MESH


def iota(shape, dim):
    return lax.broadcasted_iota(jnp.int32, shape, dim)


def one_hot(mask):
    return jnp.where(mask, F32(1), F32(0)).astype(BF)


def packed_index(pos, parity):
    tail = pos - 64 * parity
    idx = jnp.where(pos < 128, pos, tail)
    ok = (pos < 128) | ((tail >= 128) & (tail < W))
    return idx, ok


CELLS = (
    ((0, ((0, 0), (0, 1))), (0, ((1, 0), (1, 1))), (0, ((0, 2), (1, 2))), (1, ((0, 0), (0, 1)))),
    ((0, ((0, 3), (1, 3))), (1, ((1, 0), (1, 1))), (1, ((0, 2), (1, 2))), (1, ((0, 3), (1, 3)))),
)
PLACE = {
    (h, l, r): (g, q, n)
    for g in range(2) for q, (h, pair) in enumerate(CELLS[g]) for n, (l, r) in enumerate(pair)
}
STEP = (192, 96, 48)


def piece_offsets(bits):
    offs = []
    for qi in range(4):
        off = [0]
        for s in range(3):
            off.append(off[-1] + bits[(qi + s) % 4] * STEP[s])
        offs.append(off)
    return offs


def cell_at(g, qi, n):
    (l0, r0), (l1, r1) = CELLS[g][qi][1]
    return l0 + n * (l1 - l0), r0 + n * (r1 - r0)


def label_bits(y, z):
    return (((y + 1) // 2) % 2, ((z + 1) // 2) % 2, y // 2, z // 2)


def body(
    lstart, lsize, rstart, rsize, count,
    psi_hbm, left_hbm, right_hbm, lenergy, renergy, sub_hbm,
    out_hbm, proj_out,
    psi_v, gath, pp, raw, lall, rb, li, acc, subv, diag, subp,
    rs0, rs1, rs2, rs3, xrecv, pvs, pvr,
    raw_sem, psi_sem, sub_sem, out_sem,
    l_ss, l_rs, ls_ss, ls_rs, r_ss, r_rs, ro_ss, ro_rs, rf_ss, rf_rs, rs_ss, rs_rs, x_ss, x_rs,
    ag_ss, ag_rs, fw_ss, fw_rs, pv_ss, pv_rs,
):
    x = lax.axis_index("site")
    o = lax.axis_index("ops")
    c = o % 2
    y = (o // 2) % 4
    z = o // 8
    x_l = x + 1 - 2 * (x % 2)
    x_r = 3 - x
    to_l = {"site": x_l}
    to_r = {"site": x_r}
    sib = {"ops": o + 1 - 2 * c}
    to_ls = {"ops": o + 1 - 2 * c, "site": x_l}
    y_a = y + 1 - 2 * (y % 2)
    z_a = z + 1 - 2 * (z % 2)
    y_c = 3 - y_a
    z_c = 3 - z_a
    x_c = 3 - x_l
    dims = (
        {"ops": o + 2 * (y_a - y)},
        {"ops": o + 8 * (z_a - z)},
        {"ops": o + 2 * (3 - 2 * y)},
        {"ops": o + 8 * (3 - 2 * z)},
    )
    far = ({"ops": o + 2 * (y_c - y)}, {"ops": o + 8 * (z_c - z)}, {"site": x_c})
    bits = label_bits(y, z)
    offs = piece_offsets(bits)
    data = pl.ds(64, W)

    def raw_copies(m):
        buf = m % 2
        return (
            pltpu.make_async_copy(left_hbm.at[pl.ds(NS * m, NS)], raw.at[buf, 0], raw_sem.at[buf, 0]),
            pltpu.make_async_copy(right_hbm.at[pl.ds(NS * m, NS)], raw.at[buf, 1], raw_sem.at[buf, 1]),
        )

    for m in range(2):
        for cp in raw_copies(m):
            cp.start()
    psi_copy = pltpu.make_async_copy(psi_hbm, psi_v, psi_sem)
    psi_copy.start()

    pvr[...] = jnp.zeros_like(pvr)
    barrier = pltpu.get_barrier_semaphore()
    for who in (to_l, to_r, sib, to_ls, *dims, *far):
        pl.semaphore_signal(barrier, inc=1, device_id=who, device_id_type=MESH)

    def l_copy(ph, m, w):
        at = pl.ds(NS * m, NS)
        tiles = pl.ds(0, 2) if ph == 0 else pl.ds(2, 1)
        return pltpu.make_async_remote_copy(
            src_ref=lall.at[c if w == 0 else 1 - c, at, tiles], dst_ref=lall.at[3 + w, at, tiles],
            send_sem=l_ss.at[ph, m, w], recv_sem=l_rs.at[ph, m, w],
            device_id=to_l if w == 0 else to_ls, device_id_type=MESH)

    def ls_copy(m):
        at = pl.ds(NS * m, NS)
        return pltpu.make_async_remote_copy(
            src_ref=lall.at[1 - c, at], dst_ref=lall.at[2, at], send_sem=ls_ss.at[m], recv_sem=ls_rs.at[m],
            device_id=sib, device_id_type=MESH)

    def r_copy(p, m):
        at = pl.ds(NS * m, NS)
        return pltpu.make_async_remote_copy(
            src_ref=rb.at[0, p, at, :, data, :], dst_ref=rb.at[2, p, at, :, data, :],
            send_sem=r_ss.at[p, m], recv_sem=r_rs.at[p, m], device_id=to_r, device_id_type=MESH)

    def ro_copy(m):
        at = pl.ds(NS * m, NS)
        return pltpu.make_async_remote_copy(
            src_ref=rb.at[0, :, at, :, data, :], dst_ref=rb.at[1, :, at, :, data, :],
            send_sem=ro_ss.at[m], recv_sem=ro_rs.at[m], device_id=sib, device_id_type=MESH)

    def rf_copy(p, m):
        at = pl.ds(NS * m, NS)
        return pltpu.make_async_remote_copy(
            src_ref=rb.at[2, p, at, :, data, :], dst_ref=rb.at[3, p, at, :, data, :],
            send_sem=rf_ss.at[p, m], recv_sem=rf_rs.at[p, m], device_id=sib, device_id_type=MESH)

    def pack(m):
        buf = m % 2

        def one(k, carry):
            s = k // 2
            p = k % 2
            slot = NS * m + s
            row = iota((W, 128), 0)
            live = slot < count[0]
            keep = []
            for n in range(2):
                size = jnp.where(live, lsize[x * 4 + 2 * n + p], 0)
                keep.append(one_hot(row < size))
            ev = raw[buf, 0, s, p]
            od = raw[buf, 0, s, 2 + p]
            lall[p, slot, 0] = ev[:, :128] * keep[0]
            lall[p, slot, 2] = od[:, :128] * keep[1]
            lall[p, slot, 1] = jnp.concatenate(
                [ev[:, 128:] * keep[0][:, :64], od[:, 128:] * keep[1][:, :64]], axis=1)
            ev = raw[buf, 1, s, 2 * p]
            od = raw[buf, 1, s, 2 * p + 1]
            rb[0, p, slot, 0, data, :] = ev[:, :128]
            rb[0, p, slot, 1, data, :] = od[:, :128]
            rb[0, p, slot, 2, data, :] = jnp.concatenate([ev[:, 128:], od[:, 128:]], axis=1)
            return carry

        lax.fori_loop(0, 2 * NS, one, 0)

    for m in range(NC):
        for cp in raw_copies(m):
            cp.wait()
        pack(m)
        if m == 0:
            pl.semaphore_wait(barrier, 11)
        if m + 2 < NC:
            for cp in raw_copies(m + 2):
                cp.start()
        for w in range(2):
            l_copy(0, m, w).start()
        r_copy(0, m).start()
        ls_copy(m).start()
        ro_copy(m).start()
    for m in range(NC):
        for w in range(2):
            l_copy(1, m, w).start()
        r_copy(1, m).start()

    def piece(g, qi):
        off = offs[qi][3]
        n = off // W
        l, r = cell_at(g, qi, n)
        return 2 * l + c, off - n * W, r

    def sub_copy(g, qi, k):
        i, a0, r = piece(g, qi)
        return pltpu.make_async_copy(
            sub_hbm.at[k, i, pl.ds(pl.multiple_of(a0, 16), 48), :],
            subv.at[g * 4 + qi, k], sub_sem.at[g * 4 + qi, k])

    for g in range(2):
        for qi in range(4):
            for k in range(2):
                sub_copy(g, qi, k).start()

    zrow = jnp.zeros((SLOTS, 3, 64, 128), BF)

    def clear(k, carry):
        for start in (0, 256):
            rb[k // 2, k % 2, :, :, pl.ds(start, 64), :] = zrow
        acc[k // 4, k % 4] = jnp.zeros((384, 384), F32)
        return carry

    lax.fori_loop(0, 8, clear, 0)

    psi_copy.wait()

    def row_hot(q, first, rows, half):
        rs = lstart[q]
        t0 = jnp.minimum(rs // 16, BOND // 16 - 16)
        pos = iota((rows, 256), 0) + first
        if half is None:
            idx, ok = pos, pos < W
        else:
            idx, ok = packed_index(pos, half)
        ok = ok & (idx < lsize[q])
        return t0, one_hot(ok & (iota((rows, 256), 1) == idx + (rs - t0 * 16)))

    def put_rows(at, rows, t0, hot):
        for n in range(4):
            win = jnp.concatenate([psi_v[t0 + k, :, pl.ds(n * 512, 512)] for k in range(16)], axis=0)
            got = jnp.dot(hot, win, preferred_element_type=F32).astype(BF)
            for k in range(4):
                gath[n * 4 + k, pl.ds(at, rows), :] = got[:, k * 128:(k + 1) * 128]

    def rows_of(i, carry):
        q = jnp.where(i < 2, x, x_l) * 4 + 2 * (i % 2) + c
        t0, hot = row_hot(q, 0, 256, i % 2)
        put_rows(pl.multiple_of(i * 256, 256), 256, t0, hot)
        return carry

    lax.fori_loop(0, 4, rows_of, 0)

    def cols_of(j, carry):
        q = jnp.where(j < 4, x * 4 + j, x_r * 4 + j - 4)
        cs = rstart[q]
        ct = jnp.minimum(cs // 128, BOND // 128 - 3)
        idx, ok = packed_index(iota((384, 256), 1), q % 2)
        ok = ok & (idx < rsize[q])
        hot = one_hot(ok & (iota((384, 256), 0) == idx + (cs - ct * 128)))
        for m in range(2):
            win = jnp.concatenate([gath[ct + k, pl.ds(m * 512, 512), :] for k in range(3)], axis=1)
            pp[j, pl.ds(m * 512, 512), :] = jnp.dot(win, hot, preferred_element_type=F32).astype(BF)
        return carry

    lax.fori_loop(0, 8, cols_of, 0)

    def own_rows():
        re = renergy[...]
        hi = re.astype(BF)
        rem = re - hi.astype(F32)
        mid = rem.astype(BF)
        low = (rem - mid.astype(F32)).astype(BF)
        rows16 = iota((16, BOND), 0)
        er3 = jnp.where(rows16 == 0, hi.astype(F32),
                        jnp.where(rows16 == 1, mid.astype(F32),
                                  jnp.where(rows16 == 2, low.astype(F32), F32(0)))).astype(BF)
        for t in range(16):
            for qi in range(4):
                gath[t, pl.ds(qi * 160 + 144, 16), :] = er3[:, t * 128:(t + 1) * 128]
        for g in range(2):
            for qi in range(4):
                n8 = g * 4 + qi
                at = qi * 160
                i, a0, r = piece(g, qi)
                q = x * 4 + i
                t0, hot = row_hot(q, a0, 48, None)
                put_rows(at, 48, t0, hot)
                for k in range(2):
                    sub_copy(g, qi, k).wait()
                    for t in range(16):
                        gath[t, pl.ds(at + 48 + 48 * k, 48), :] = subv[n8, k, :, pl.ds(t * 128, 128)]
                xt = x if CELLS[g][qi][0] == 0 else x_l
                site = xt + (r // 2) * (3 - 2 * xt)
                total = None
                for par in range(2):
                    qr = site * 4 + 2 * (r % 2) + par
                    cs = rstart[qr]
                    ct = jnp.minimum(cs // 128, BOND // 128 - 3)
                    j = iota((384, 384), 1) - W * par
                    hot2 = one_hot((j >= 0) & (j < W) & (j < rsize[qr])
                                   & (iota((384, 384), 0) == j + (cs - ct * 128)))
                    win = jnp.concatenate([gath[ct + k, pl.ds(at, 160), :] for k in range(3)], axis=1)
                    part = jnp.dot(win, hot2, preferred_element_type=F32)
                    total = part if total is None else total + part
                lt = jnp.minimum(lstart[q] // 128, BOND // 128 - 3)
                shift = lstart[q] - lt * 128 + a0
                pick = iota((48, 384), 1) == iota((48, 384), 0) + shift
                lrow = jnp.concatenate([lenergy[lt + k] for k in range(3)], axis=1)
                el = jnp.sum(jnp.where(pick, lrow, F32(0)), axis=1, keepdims=True)
                er = total[144:145] + total[145:146] + total[146:147]
                diag[n8] = (el + er) * total[:48]
                subp[n8, 0] = total[48:96]
                subp[n8, 1] = total[96:144]

    left_at = {(0, 0): c, (0, 1): 2, (1, 0): 3, (1, 1): 4}

    def product(m, w, r, lefts):
        slots = pl.ds(NS * m, NS)
        side = (0 if r < 2 else 2) + w
        for par in range(2):
            j = 2 * r + par
            for n, (h, l) in enumerate(lefts):
                src = left_at[(h, w)]
                lhs = jnp.concatenate([lall[src, slots, 2 * l].reshape(NS * W, 128),
                                       lall[src, slots, 1].reshape(NS * W, 128)], axis=1)
                img = jnp.dot(lhs, pp[j, pl.ds((2 * h + l) * 256, 256), :],
                              preferred_element_type=F32).astype(BF)
                for s in range(NS):
                    li[pl.ds(n * W, W), pl.ds(s * 256, 256)] = img[s * W:(s + 1) * W]
            rows = pl.ds(64 - 64 * par, 256)
            rhs = jnp.concatenate(
                [rb[side, r % 2, NS * m + s, k, rows, :] for s in range(NS) for k in (par, 2)], axis=1)
            lanes = pl.ds(128 * par, 256)
            res = lax.dot_general(li[pl.ds(0, len(lefts) * W), :], rhs, (((1,), (1,)), ((), ())),
                                  preferred_element_type=F32)
            for n, (h, l) in enumerate(lefts):
                g, q, cell = PLACE[(h, l, r)]
                acc[g, q, pl.ds(cell * W, W), lanes] += res[n * W:(n + 1) * W]

    def arrive(p, m):
        r_copy(p, m).wait()
        rf_copy(p, m).start()
        for w in range(2):
            l_copy(p, m, w).wait()

    rsb = (rs0, rs1, rs2, rs3)

    def rs_copy(g, qi, s):
        d = (qi + s) % 4
        if s < 3:
            rows = STEP[s]
            first = offs[qi][s] + (1 - bits[d]) * rows
        else:
            rows, first = 48, offs[qi][3]
        return pltpu.make_async_remote_copy(
            src_ref=acc.at[g, qi, pl.ds(pl.multiple_of(first, 16), rows), :],
            dst_ref=rsb[s].at[g, qi], send_sem=rs_ss.at[g, qi, s], recv_sem=rs_rs.at[g, qi, s],
            device_id=dims[d], device_id_type=MESH)

    def add_rows(g, qi, first, src, src_first, rows):
        def step(k, carry):
            at = pl.ds(pl.multiple_of(first + k * 48, 16), 48)
            acc[g, qi, at, :] += src[pl.ds(pl.multiple_of(src_first + k * 48, 16), 48), :]
            return carry

        lax.fori_loop(0, rows // 48, step, 0)

    def x_copy(g, qi):
        return pltpu.make_async_remote_copy(
            src_ref=acc.at[g, qi, pl.ds(pl.multiple_of(offs[qi][3], 16), 48), :], dst_ref=xrecv.at[g, qi],
            send_sem=x_ss.at[g, qi], recv_sem=x_rs.at[g, qi], device_id=to_l, device_id_type=MESH)

    def reduce_step(g, s):
        for qi in range(4):
            rs_copy(g, qi, s).wait_recv()
            if s == 3:
                rs_copy(g, qi, 3).wait_send()
                add_rows(g, qi, offs[qi][3], rs3.at[g, qi], 0, 48)
                if CELLS[g][qi][0] == 1:
                    x_copy(g, qi).start()
            else:
                add_rows(g, qi, offs[qi][s + 1], rsb[s].at[g, qi], 0, STEP[s])
                rs_copy(g, qi, s + 1).start()

    def rows_at(g, qi, first, rows, core):
        n = first // W
        l, r = cell_at(g, qi, n)
        tile = CELLS[g][qi][0] * 48 + (2 * l + core) * 12 + (first - n * W) // 16
        return pl.ds(tile, rows // 16), pl.ds(pl.multiple_of(r * 384, 128), 384)

    def ag_copy(g, qi, s, mine):
        d = (qi + s) % 4
        first = offs[qi][s + 1] if mine else offs[qi][s] + (1 - bits[d]) * STEP[s]
        at, lanes = rows_at(g, qi, first, STEP[s], c)
        return pltpu.make_async_remote_copy(
            src_ref=psi_v.at[at, :, lanes], dst_ref=psi_v.at[at, :, lanes],
            send_sem=ag_ss.at[g, qi, s], recv_sem=ag_rs.at[g, qi, s],
            device_id=dims[d], device_id_type=MESH)

    def fw_copy(g, qi, s, core):
        if s == 3:
            first, rows = offs[qi][3], 48
        else:
            first, rows = offs[qi][s] + (1 - bits[(qi + s) % 4]) * STEP[s], STEP[s]
        at, lanes = rows_at(g, qi, first, rows, core)
        return pltpu.make_async_remote_copy(
            src_ref=psi_v.at[at, :, lanes], dst_ref=psi_v.at[at, :, lanes],
            send_sem=fw_ss.at[g, qi, s], recv_sem=fw_rs.at[g, qi, s],
            device_id=sib, device_id_type=MESH)

    sums = [jnp.zeros((1, 1), F32), jnp.zeros((1, 1), F32)]

    def finish(g, h):
        for qi in range(4):
            if CELLS[g][qi][0] != h:
                continue
            off = offs[qi][3]
            if h == 0:
                part = acc[g, qi, pl.ds(pl.multiple_of(off, 16), 48), :]
            else:
                x_copy(g, qi).wait_recv()
                part = xrecv[g, qi]
            full = part + diag[g * 4 + qi]
            at, lanes = rows_at(g, qi, off, 48, c)
            psi_v[at, :, lanes] = full.astype(BF).reshape(3, 16, 384)
            ag_copy(g, qi, 2, True).start()
            fw_copy(g, qi, 3, c).start()
            weight = (1 - bits[(qi + 3) % 4]).astype(F32)
            for k in range(2):
                sums[k] = sums[k] + weight * jnp.sum(full * subp[g * 4 + qi, k], keepdims=True)

    def gather_step(g, s, h=None):
        for qi in range(4):
            if h is not None and CELLS[g][qi][0] != h:
                continue
            ag_copy(g, qi, s, False).wait_recv()
            if s > 0:
                ag_copy(g, qi, s - 1, True).start()
            fw_copy(g, qi, s, c).start()

    def step0(m, carry):
        for w in range(2):
            if w == 1:
                ls_copy(m).wait_recv()
                ro_copy(m).wait_recv()
            for r in range(2):
                product(m, w, r, ((0, 0), (0, 1)))
        return carry

    lax.fori_loop(0, NC, step0, 0)

    def step1(m, carry):
        arrive(0, m)
        for w in range(2):
            if w == 1:
                rf_copy(0, m).wait_recv()
            for r in range(2):
                product(m, w, r, ((1, 0),))
            product(m, w, 2, ((0, 0), (0, 1), (1, 0)))
        return carry

    lax.fori_loop(0, NC, step1, 0)
    for qi in range(4):
        rs_copy(0, qi, 0).start()
    own_rows()

    def first_half(m):
        arrive(1, m)
        for w in range(2):
            for r in range(3):
                product(m, w, r, ((1, 1),))

    def second_half(m):
        for w in range(2):
            if w == 1:
                rf_copy(1, m).wait_recv()
            product(m, w, 3, ((0, 0), (0, 1), (1, 0), (1, 1)))

    first_half(0)
    second_half(0)
    reduce_step(0, 0)
    first_half(1)
    second_half(1)
    reduce_step(0, 1)
    first_half(2)
    reduce_step(0, 2)
    second_half(2)
    reduce_step(0, 3)
    finish(0, 0)
    first_half(3)
    for qi in (1, 2):
        rs_copy(1, qi, 0).start()
    second_half(3)
    for qi in (0, 3):
        rs_copy(1, qi, 0).start()
    finish(0, 1)
    gather_step(0, 2)
    gather_step(0, 1)
    reduce_step(1, 0)
    gather_step(0, 0)
    reduce_step(1, 1)
    reduce_step(1, 2)
    reduce_step(1, 3)
    finish(1, 0)
    finish(1, 1)

    lane = iota((8, 128), 1)
    pvs[0] = jnp.where(lane == 0, sums[0], jnp.where(lane == 1, sums[1], F32(0)))
    rounds = (
        (c, ((sib, 1 - c),)),
        (y, ((dims[0], y_a), (dims[2], 3 - y), (far[0], y_c))),
        (z, ((dims[1], z_a), (dims[3], 3 - z), (far[1], z_c))),
        (x, ((to_l, x_l), (to_r, x_r), (far[2], x_c))),
    )

    def pv_copy(n, i, slot):
        return pltpu.make_async_remote_copy(
            src_ref=pvs.at[n], dst_ref=pvr.at[n, slot], send_sem=pv_ss.at[n, i], recv_sem=pv_rs.at[n, slot],
            device_id=rounds[n][1][i][0], device_id_type=MESH)

    def pv_send(n):
        me, others = rounds[n]
        for i in range(len(others)):
            pv_copy(n, i, me).start()
        pvr[n, me] = pvs[n]

    def pv_sum(n):
        me, others = rounds[n]
        for i, (who, slot) in enumerate(others):
            pv_copy(n, i, slot).wait_recv()
        pvs[n + 1] = (pvr[n, 0] + pvr[n, 1]) + (pvr[n, 2] + pvr[n, 3])

    def o_copy(k, core):
        return [pltpu.make_async_copy(
            psi_v.at[pl.ds((k // 4) * 48 + (2 * l + core) * 12, 12), :, pl.ds((k % 4) * 384, 384)],
            out_hbm.at[k, pl.ds((2 * l + core) * 12, 12)], out_sem.at[k, core, l]) for l in range(2)]

    pv_send(0)
    for n, s in enumerate((2, 1, 0)):
        gather_step(1, s)
        pv_sum(n)
        pv_send(n + 1)
    for k in range(8):
        for cp in o_copy(k, c):
            cp.start()
    for g in range(2):
        for s in (3, 2, 1, 0):
            for qi in range(4):
                fw_copy(g, qi, s, 1 - c).wait_recv()
    for k in range(8):
        for cp in o_copy(k, 1 - c):
            cp.start()
    pv_sum(3)
    proj_out[...] = pvs[4]
    for g in range(2):
        for qi in range(4):
            for s in range(3):
                rs_copy(g, qi, s).wait_send()
                ag_copy(g, qi, s, True).wait_send()
            for s in range(4):
                fw_copy(g, qi, s, c).wait_send()
            if CELLS[g][qi][0] == 1:
                x_copy(g, qi).wait_send()
    for m in range(NC):
        ls_copy(m).wait_send()
        ro_copy(m).wait_send()
        for p in range(2):
            rf_copy(p, m).wait_send()
    for n in range(4):
        for i in range(len(rounds[n][1])):
            pv_copy(n, i, rounds[n][0]).wait_send()
    for k in range(8):
        for core in (c, 1 - c):
            for cp in o_copy(k, core):
                cp.wait()


def compact_body(rstart, rsize, src, out):
    x = lax.axis_index("site")
    k = pl.program_id(0)
    x_l = x + 1 - 2 * (x % 2)

    @pl.when(k == 0)
    def _():
        out[...] = jnp.zeros_like(out)

    xt = jnp.where(k // 4 == 0, x, x_l)
    site = xt + ((k // 2) % 2) * (3 - 2 * xt)
    q = site * 4 + 2 * (k % 2)
    start = rstart[q]
    base = pl.multiple_of(jnp.minimum((start // 128) * 128, BOND - 512), 128)
    j = iota((384, 512), 0)
    odd = j >= W
    idx = jnp.where(odd, j - W, j)
    size = jnp.where(odd, rsize[q + 1], rsize[q])
    first = jnp.where(odd, rstart[q + 1], start) - base
    hot = one_hot((idx < size) & (iota((384, 512), 1) == idx + first))
    out[:, pl.ds(base, 512)] += jnp.dot(src[0], hot, preferred_element_type=F32).astype(BF)


def sector_tables(sector_ids, sectors):
    labels = jnp.arange(sectors, dtype=jnp.int32)
    starts = jnp.sum((sector_ids[None, :] < labels[:, None]).astype(jnp.int32), axis=1)
    sizes = jnp.sum((sector_ids[None, :] == labels[:, None]).astype(jnp.int32), axis=1)
    return starts, sizes


def local(wavefunction, left_blocks, right_blocks, left_sector, right_sector, term_count,
          left_energy, right_energy, subspace):
    lstart, lsize = sector_tables(left_sector, 16)
    rstart, rsize = sector_tables(right_sector, 16)
    smem = pl.BlockSpec(memory_space=pltpu.SMEM)
    vmem = pl.BlockSpec(memory_space=pltpu.VMEM)
    hbm = pl.BlockSpec(memory_space=pl.ANY)
    dma = pltpu.SemaphoreType.DMA
    slabs, proj = pl.pallas_call(
        body,
        out_shape=(jax.ShapeDtypeStruct((8, 48, 16, 384), BF), jax.ShapeDtypeStruct((8, 128), F32)),
        in_specs=[smem] * 5 + [hbm] * 3 + [vmem] * 2 + [hbm],
        out_specs=(hbm, vmem),
        scratch_shapes=[
            pltpu.VMEM((BOND // 16, 16, BOND), BF),
            pltpu.VMEM((16, 1024, 128), BF),
            pltpu.VMEM((8, 1024, 256), BF),
            pltpu.VMEM((2, 2, NS, 4, W, W), BF),
            pltpu.VMEM((5, SLOTS, 3, W, 128), BF),
            pltpu.VMEM((4, 2, SLOTS, 3, 320, 128), BF),
            pltpu.VMEM((768, NS * 256), BF),
            pltpu.VMEM((2, 4, 384, 384), F32),
            pltpu.VMEM((8, 2, 48, BOND), BF),
            pltpu.VMEM((8, 48, 384), F32),
            pltpu.VMEM((8, 2, 48, 384), F32),
            pltpu.VMEM((2, 4, 192, 384), F32),
            pltpu.VMEM((2, 4, 96, 384), F32),
            pltpu.VMEM((2, 4, 48, 384), F32),
            pltpu.VMEM((2, 4, 48, 384), F32),
            pltpu.VMEM((2, 4, 48, 384), F32),
            pltpu.VMEM((5, 8, 128), F32),
            pltpu.VMEM((4, 4, 8, 128), F32),
            dma((2, 2)), dma, dma((8, 2)), dma((8, 2, 2)),
            dma((2, NC, 2)), dma((2, NC, 2)), dma((NC,)), dma((NC,)), dma((2, NC)), dma((2, NC)),
            dma((NC,)), dma((NC,)), dma((2, NC)), dma((2, NC)),
            dma((2, 4, 4)), dma((2, 4, 4)), dma((2, 4)), dma((2, 4)),
            dma((2, 4, 3)), dma((2, 4, 3)), dma((2, 4, 4)), dma((2, 4, 4)), dma((4, 3)), dma((4, 4)),
        ],
        compiler_params=pltpu.CompilerParams(
            collective_id=0, has_side_effects=True, vmem_limit_bytes=67043328),
        name="exchange",
    )(lstart, lsize, rstart, rsize, term_count, wavefunction.reshape(BOND // 16, 16, BOND),
      left_blocks, right_blocks, left_energy.reshape(16, 1, 128), right_energy.reshape(1, BOND), subspace)
    sigma = pl.pallas_call(
        compact_body,
        grid=(8,),
        out_shape=jax.ShapeDtypeStruct((768, BOND), BF),
        in_specs=[smem, smem, pl.BlockSpec((1, 768, 384), lambda k: (k, 0, 0))],
        out_specs=pl.BlockSpec((768, BOND), lambda k: (0, 0)),
        name="compact",
    )(rstart, rsize, slabs.reshape(8, 768, 384))
    return sigma.reshape(4, W, BOND), proj[0, :2]


def solution(mesh):
    in_specs = (P(), P("ops", "site", None, None), P("ops", "site", None, None), P(), P(), P("ops"),
                P(), P(), P(None, "site", None, None))
    out_specs = (P("site", None, None), P())
    return jax.shard_map(local, mesh=mesh, in_specs=in_specs, out_specs=out_specs, check_vma=False)
```

time: 150 us -> 136 us (0.907)
  Pallas kernels: 144 us -> 132 us
    pallas_call x2 -> x1, Pallas kernels: 135 us -> 122 us  [local(): pl.pallas_call(body, out_shape=(jax.ShapeDtypeStruct((8, 48, 16, 384), BF...]
where the time goes in v4:
time: 136 us
  Pallas kernels  132 us (97%)
  other arithmetic  1.49 us (1%)
    pallas_call x1, Pallas kernels, local(): pl.pallas_call(body, out_shape=(jax.ShapeDtypeStruct((8, 48, 16, 384), BF...  122 us
    pallas_call x1, Pallas kernels, local(): pl.pallas_call(compact_body, grid=(8,), out_shape=jax.ShapeDtypeStruct((7...  9.5 us

profile of v4, /device:TPU:1, one launch (start us, length us, event | category | flops | bytes accessed | tf_op | source)
XLA Modules:
  0.0 135.8 jit_solution(1998357381069785752)
XLA Ops:
  1.3 1.5 %convert_reduce_fusion = (s32[16]{0:T(128)}, s32[16]{0:T(128)}, s32[16]{0:T(128)}, s32[16]{0:T(128)}) fusion(s32[2048]{0:T(1024)} %param.12, s32[2048]{0:T(1024)} %param.13), kind=kLoop, calls=%fused_computation | loop fusion | flops 393152 | bytes 16640 | tf_op jit(solution)/shard_map/reduce_sum | solution.py:603
  2.8 122.3 %exchange.1 = (bf16[8,48,16,384]{3,2,1,0:T(8,128)(2,1)}, f32[8,128]{1,0:T(8,128)}) custom-call(s32[16]{0:T(128)} %get-tuple-element.7.lstart, s32[16]{0:T(128)} %get-tuple-element.6.lsize, s32[16]{0:T(128)} %get-tuple-element.10.rstart, s32[16]{0:T(128)} %get-tuple-element.11.rsize, s32[1]{0:T(128)S(6)} %copy.11.count, bf16[128,16,2048]{2,1,0:T(8,128)(2,1)} %bitcast.7, ...), custom_call_target="tpu_custom_call" | custom-call | tf_op jit(solution)/shard_map/exchange/pallas_call | solution.py:615
  125.1 9.5 %compact.1 = bf16[768,2048]{1,0:T(8,128)(2,1)} custom-call(s32[16]{0:T(128)} %get-tuple-element.10.rstart, s32[16]{0:T(128)} %get-tuple-element.11.rsize, bf16[8,768,384]{2,1,0:T(8,128)(2,1)} %bitcast.8), custom_call_target="tpu_custom_call" | custom-call | tf_op jit(solution)/shard_map/compact/pallas_call | solution.py:650
  134.6 1.2 slice_bitcast_fusion

commit v5 on v4

--- a/solution.py
+++ b/solution.py
@@ -31,28 +31,35 @@
 
 
 CELLS = (
-    ((0, ((0, 0), (0, 1))), (0, ((1, 0), (1, 1))), (0, ((0, 2), (1, 2))), (1, ((0, 0), (0, 1)))),
+    ((0, ((0, 0),)), (0, ((0, 1),)), (0, ((1, 0),)), (0, ((1, 1),))),
+    ((0, ((0, 2),)), (0, ((1, 2),)), (1, ((0, 0),)), (1, ((0, 1),))),
     ((0, ((0, 3), (1, 3))), (1, ((1, 0), (1, 1))), (1, ((0, 2), (1, 2))), (1, ((0, 3), (1, 3)))),
 )
+CHUNKS = len(CELLS)
+BASE = (0, 4, 8)
 PLACE = {
-    (h, l, r): (g, q, n)
-    for g in range(2) for q, (h, pair) in enumerate(CELLS[g]) for n, (l, r) in enumerate(pair)
+    (h, l, r): BASE[g] + q * len(cells) + n
+    for g in range(CHUNKS) for q, (h, cells) in enumerate(CELLS[g]) for n, (l, r) in enumerate(cells)
 }
-STEP = (192, 96, 48)
+STEPS = ((96, 48), (96, 48), (192, 96, 48))
+PARTS = (((0, 384),), ((0, 384),), ((0, 256), (256, 128)))
 
 
 def piece_offsets(bits):
     offs = []
-    for qi in range(4):
-        off = [0]
-        for s in range(3):
-            off.append(off[-1] + bits[(qi + s) % 4] * STEP[s])
-        offs.append(off)
+    for g in range(CHUNKS):
+        offs.append([])
+        for qi in range(4):
+            off = [0]
+            for s, rows in enumerate(STEPS[g]):
+                off.append(off[-1] + bits[(qi + s) % 4] * rows)
+            offs[g].append(off)
     return offs
 
 
 def cell_at(g, qi, n):
-    (l0, r0), (l1, r1) = CELLS[g][qi][1]
+    cells = CELLS[g][qi][1]
+    (l0, r0), (l1, r1) = cells[0], cells[-1]
     return l0 + n * (l1 - l0), r0 + n * (r1 - r0)
 
 
@@ -65,7 +72,7 @@
     psi_hbm, left_hbm, right_hbm, lenergy, renergy, sub_hbm,
     out_hbm, proj_out,
     psi_v, gath, pp, raw, lall, rb, li, acc, subv, diag, subp,
-    rs0, rs1, rs2, rs3, xrecv, pvs, pvr,
+    rs0, rs1, rs2, rs3, rs4, xrecv, pvs, pvr,
     raw_sem, psi_sem, sub_sem, out_sem,
     l_ss, l_rs, ls_ss, ls_rs, r_ss, r_rs, ro_ss, ro_rs, rf_ss, rf_rs, rs_ss, rs_rs, x_ss, x_rs,
     ag_ss, ag_rs, fw_ss, fw_rs, pv_ss, pv_rs,
@@ -195,7 +202,7 @@
         r_copy(1, m).start()
 
     def piece(g, qi):
-        off = offs[qi][3]
+        off = offs[g][qi][-1]
         n = off // W
         l, r = cell_at(g, qi, n)
         return 2 * l + c, off - n * W, r
@@ -206,7 +213,7 @@
             sub_hbm.at[k, i, pl.ds(pl.multiple_of(a0, 16), 48), :],
             subv.at[g * 4 + qi, k], sub_sem.at[g * 4 + qi, k])
 
-    for g in range(2):
+    for g in range(CHUNKS):
         for qi in range(4):
             for k in range(2):
                 sub_copy(g, qi, k).start()
@@ -216,7 +223,8 @@
     def clear(k, carry):
         for start in (0, 256):
             rb[k // 2, k % 2, :, :, pl.ds(start, 64), :] = zrow
-        acc[k // 4, k % 4] = jnp.zeros((384, 384), F32)
+        acc[2 * k] = jnp.zeros((W, 384), F32)
+        acc[2 * k + 1] = jnp.zeros((W, 384), F32)
         return carry
 
     lax.fori_loop(0, 8, clear, 0)
@@ -276,7 +284,7 @@
         for t in range(16):
             for qi in range(4):
                 gath[t, pl.ds(qi * 160 + 144, 16), :] = er3[:, t * 128:(t + 1) * 128]
-        for g in range(2):
+        for g in range(CHUNKS):
             for qi in range(4):
                 n8 = g * 4 + qi
                 at = qi * 160
@@ -333,8 +341,7 @@
             res = lax.dot_general(li[pl.ds(0, len(lefts) * W), :], rhs, (((1,), (1,)), ((), ())),
                                   preferred_element_type=F32)
             for n, (h, l) in enumerate(lefts):
-                g, q, cell = PLACE[(h, l, r)]
-                acc[g, q, pl.ds(cell * W, W), lanes] += res[n * W:(n + 1) * W]
+                acc[PLACE[(h, l, r)], :, lanes] += res[n * W:(n + 1) * W]
 
     def arrive(p, m):
         r_copy(p, m).wait()
@@ -342,100 +349,128 @@
         for w in range(2):
             l_copy(p, m, w).wait()
 
-    rsb = (rs0, rs1, rs2, rs3)
-
-    def rs_copy(g, qi, s):
+    def landing(g, qi, s):
+        steps = STEPS[g]
+        if s == 3:
+            return rs3.at[g, qi], 48, True
+        if s == len(steps):
+            return rs4.at[g, qi], 48, True
+        rows = steps[s]
+        return {192: rs0.at[qi], 96: rs1.at[g, qi], 48: rs2.at[g, qi]}[rows], rows, False
+
+    def lanes_of(g, pt, first=0):
+        start, width = PARTS[g][pt]
+        return pl.ds(pl.multiple_of(first + start, 128), width)
+
+    def strip(g, qi, first, rows):
+        n = first // W
+        return BASE[g] + qi * len(CELLS[g][qi][1]) + n, pl.ds(pl.multiple_of(first - n * W, 16), rows)
+
+    def rs_copy(g, qi, s, pt):
         d = (qi + s) % 4
-        if s < 3:
-            rows = STEP[s]
-            first = offs[qi][s] + (1 - bits[d]) * rows
-        else:
-            rows, first = 48, offs[qi][3]
-        return pltpu.make_async_remote_copy(
-            src_ref=acc.at[g, qi, pl.ds(pl.multiple_of(first, 16), rows), :],
-            dst_ref=rsb[s].at[g, qi], send_sem=rs_ss.at[g, qi, s], recv_sem=rs_rs.at[g, qi, s],
+        dst, rows, whole = landing(g, qi, s)
+        first = offs[g][qi][-1] if whole else offs[g][qi][s] + (1 - bits[d]) * rows
+        n, at = strip(g, qi, first, rows)
+        return pltpu.make_async_remote_copy(
+            src_ref=acc.at[n, at, lanes_of(g, pt)], dst_ref=dst.at[:, lanes_of(g, pt)],
+            send_sem=rs_ss.at[g, qi, s, pt], recv_sem=rs_rs.at[g, qi, s, pt],
             device_id=dims[d], device_id_type=MESH)
 
-    def add_rows(g, qi, first, src, src_first, rows):
+    def add_rows(g, qi, first, src, rows, pt):
+        lanes = lanes_of(g, pt)
+        n = first // W
+        row = first - n * W
+        n = BASE[g] + qi * len(CELLS[g][qi][1]) + n
+
         def step(k, carry):
-            at = pl.ds(pl.multiple_of(first + k * 48, 16), 48)
-            acc[g, qi, at, :] += src[pl.ds(pl.multiple_of(src_first + k * 48, 16), 48), :]
+            at = pl.ds(pl.multiple_of(row + k * 48, 16), 48)
+            acc[n, at, lanes] += src[pl.ds(pl.multiple_of(k * 48, 16), 48), lanes]
             return carry
 
         lax.fori_loop(0, rows // 48, step, 0)
 
-    def x_copy(g, qi):
-        return pltpu.make_async_remote_copy(
-            src_ref=acc.at[g, qi, pl.ds(pl.multiple_of(offs[qi][3], 16), 48), :], dst_ref=xrecv.at[g, qi],
-            send_sem=x_ss.at[g, qi], recv_sem=x_rs.at[g, qi], device_id=to_l, device_id_type=MESH)
-
-    def reduce_step(g, s):
+    def x_copy(g, qi, pt):
+        lanes = lanes_of(g, pt)
+        n, at = strip(g, qi, offs[g][qi][-1], 48)
+        return pltpu.make_async_remote_copy(
+            src_ref=acc.at[n, at, lanes], dst_ref=xrecv.at[g, qi, :, lanes],
+            send_sem=x_ss.at[g, qi, pt], recv_sem=x_rs.at[g, qi, pt], device_id=to_l, device_id_type=MESH)
+
+    def reduce_step(g, s, pt=0):
         for qi in range(4):
-            rs_copy(g, qi, s).wait_recv()
-            if s == 3:
-                rs_copy(g, qi, 3).wait_send()
-                add_rows(g, qi, offs[qi][3], rs3.at[g, qi], 0, 48)
-                if CELLS[g][qi][0] == 1:
-                    x_copy(g, qi).start()
-            else:
-                add_rows(g, qi, offs[qi][s + 1], rsb[s].at[g, qi], 0, STEP[s])
-                rs_copy(g, qi, s + 1).start()
-
-    def rows_at(g, qi, first, rows, core):
+            src, rows, whole = landing(g, qi, s)
+            rs_copy(g, qi, s, pt).wait_recv()
+            if whole:
+                rs_copy(g, qi, s, pt).wait_send()
+            add_rows(g, qi, offs[g][qi][-1] if whole else offs[g][qi][s + 1], src, rows, pt)
+            if s < 3:
+                rs_copy(g, qi, s + 1, pt).start()
+            elif CELLS[g][qi][0] == 1:
+                x_copy(g, qi, pt).start()
+
+    def rows_at(g, qi, first, rows, core, pt):
         n = first // W
         l, r = cell_at(g, qi, n)
         tile = CELLS[g][qi][0] * 48 + (2 * l + core) * 12 + (first - n * W) // 16
-        return pl.ds(tile, rows // 16), pl.ds(pl.multiple_of(r * 384, 128), 384)
-
-    def ag_copy(g, qi, s, mine):
+        return pl.ds(tile, rows // 16), lanes_of(g, pt, r * 384)
+
+    def ag_copy(g, qi, s, mine, pt):
         d = (qi + s) % 4
-        first = offs[qi][s + 1] if mine else offs[qi][s] + (1 - bits[d]) * STEP[s]
-        at, lanes = rows_at(g, qi, first, STEP[s], c)
+        rows = STEPS[g][s]
+        first = offs[g][qi][s + 1] if mine else offs[g][qi][s] + (1 - bits[d]) * rows
+        at, lanes = rows_at(g, qi, first, rows, c, pt)
         return pltpu.make_async_remote_copy(
             src_ref=psi_v.at[at, :, lanes], dst_ref=psi_v.at[at, :, lanes],
-            send_sem=ag_ss.at[g, qi, s], recv_sem=ag_rs.at[g, qi, s],
+            send_sem=ag_ss.at[g, qi, s, pt], recv_sem=ag_rs.at[g, qi, s, pt],
             device_id=dims[d], device_id_type=MESH)
 
-    def fw_copy(g, qi, s, core):
+    def fw_copy(g, qi, s, core, pt):
         if s == 3:
-            first, rows = offs[qi][3], 48
+            first, rows = offs[g][qi][-1], 48
         else:
-            first, rows = offs[qi][s] + (1 - bits[(qi + s) % 4]) * STEP[s], STEP[s]
-        at, lanes = rows_at(g, qi, first, rows, core)
+            rows = STEPS[g][s]
+            first = offs[g][qi][s] + (1 - bits[(qi + s) % 4]) * rows
+        at, lanes = rows_at(g, qi, first, rows, core, pt)
         return pltpu.make_async_remote_copy(
             src_ref=psi_v.at[at, :, lanes], dst_ref=psi_v.at[at, :, lanes],
-            send_sem=fw_ss.at[g, qi, s], recv_sem=fw_rs.at[g, qi, s],
+            send_sem=fw_ss.at[g, qi, s, pt], recv_sem=fw_rs.at[g, qi, s, pt],
             device_id=sib, device_id_type=MESH)
 
-    sums = [jnp.zeros((1, 1), F32), jnp.zeros((1, 1), F32)]
-
-    def finish(g, h):
+    totals = [jnp.zeros((48, 128), F32), jnp.zeros((48, 128), F32)]
+
+    def finish(g, h, pt=0):
+        lanes = lanes_of(g, pt)
         for qi in range(4):
             if CELLS[g][qi][0] != h:
                 continue
-            off = offs[qi][3]
+            off = offs[g][qi][-1]
             if h == 0:
-                part = acc[g, qi, pl.ds(pl.multiple_of(off, 16), 48), :]
+                n, rows = strip(g, qi, off, 48)
+                part = acc[n, rows, lanes]
             else:
-                x_copy(g, qi).wait_recv()
-                part = xrecv[g, qi]
-            full = part + diag[g * 4 + qi]
-            at, lanes = rows_at(g, qi, off, 48, c)
-            psi_v[at, :, lanes] = full.astype(BF).reshape(3, 16, 384)
-            ag_copy(g, qi, 2, True).start()
-            fw_copy(g, qi, 3, c).start()
-            weight = (1 - bits[(qi + 3) % 4]).astype(F32)
+                x_copy(g, qi, pt).wait_recv()
+                part = xrecv[g, qi, :, lanes]
+            full = part + diag[g * 4 + qi, :, lanes]
+            at, where = rows_at(g, qi, off, 48, c, pt)
+            width = PARTS[g][pt][1]
+            psi_v[at, :, where] = full.astype(BF).reshape(3, 16, width)
+            ag_copy(g, qi, len(STEPS[g]) - 1, True, pt).start()
+            fw_copy(g, qi, 3, c, pt).start()
+            weight = 1 - bits[(qi + 3) % 4]
+            if len(STEPS[g]) == 2:
+                weight = weight * (1 - bits[(qi + 2) % 4])
+            weight = weight.astype(F32)
             for k in range(2):
-                sums[k] = sums[k] + weight * jnp.sum(full * subp[g * 4 + qi, k], keepdims=True)
-
-    def gather_step(g, s, h=None):
+                prod = weight * full * subp[g * 4 + qi, k, :, lanes]
+                for t in range(width // 128):
+                    totals[k] = totals[k] + prod[:, t * 128:(t + 1) * 128]
+
+    def gather_step(g, s, pt=0):
         for qi in range(4):
-            if h is not None and CELLS[g][qi][0] != h:
-                continue
-            ag_copy(g, qi, s, False).wait_recv()
+            ag_copy(g, qi, s, False, pt).wait_recv()
             if s > 0:
-                ag_copy(g, qi, s - 1, True).start()
-            fw_copy(g, qi, s, c).start()
+                ag_copy(g, qi, s - 1, True, pt).start()
+            fw_copy(g, qi, s, c, pt).start()
 
     def step0(m, carry):
         for w in range(2):
@@ -447,6 +482,10 @@
         return carry
 
     lax.fori_loop(0, NC, step0, 0)
+    for qi in range(4):
+        rs_copy(0, qi, 0, 0).start()
+    own_rows()
+    reduce_step(0, 0)
 
     def step1(m, carry):
         arrive(0, m)
@@ -458,10 +497,12 @@
             product(m, w, 2, ((0, 0), (0, 1), (1, 0)))
         return carry
 
-    lax.fori_loop(0, NC, step1, 0)
+    lax.fori_loop(0, NC // 2, step1, 0)
+    reduce_step(0, 1)
+    lax.fori_loop(NC // 2, NC, step1, 0)
     for qi in range(4):
-        rs_copy(0, qi, 0).start()
-    own_rows()
+        rs_copy(1, qi, 0, 0).start()
+    reduce_step(0, 2)
 
     def first_half(m):
         arrive(1, m)
@@ -476,34 +517,45 @@
             product(m, w, 3, ((0, 0), (0, 1), (1, 0), (1, 1)))
 
     first_half(0)
+    reduce_step(0, 3)
+    finish(0, 0)
     second_half(0)
-    reduce_step(0, 0)
+    reduce_step(1, 0)
+    gather_step(0, 1)
     first_half(1)
     second_half(1)
-    reduce_step(0, 1)
+    reduce_step(1, 1)
+    gather_step(0, 0)
     first_half(2)
-    reduce_step(0, 2)
     second_half(2)
-    reduce_step(0, 3)
-    finish(0, 0)
+    reduce_step(1, 2)
     first_half(3)
     for qi in (1, 2):
-        rs_copy(1, qi, 0).start()
+        for pt in range(2):
+            rs_copy(2, qi, 0, pt).start()
     second_half(3)
     for qi in (0, 3):
-        rs_copy(1, qi, 0).start()
-    finish(0, 1)
-    gather_step(0, 2)
-    gather_step(0, 1)
-    reduce_step(1, 0)
-    gather_step(0, 0)
-    reduce_step(1, 1)
-    reduce_step(1, 2)
+        for pt in range(2):
+            rs_copy(2, qi, 0, pt).start()
     reduce_step(1, 3)
     finish(1, 0)
+    reduce_step(2, 0, 0)
     finish(1, 1)
+    reduce_step(2, 0, 1)
+    reduce_step(2, 1, 0)
+    gather_step(1, 1)
+    reduce_step(2, 1, 1)
+    reduce_step(2, 2, 0)
+    gather_step(1, 0)
+    reduce_step(2, 2, 1)
+    for pt in range(2):
+        reduce_step(2, 3, pt)
+    for pt in range(2):
+        finish(2, 0, pt)
+        finish(2, 1, pt)
 
     lane = iota((8, 128), 1)
+    sums = [jnp.sum(total, keepdims=True) for total in totals]
     pvs[0] = jnp.where(lane == 0, sums[0], jnp.where(lane == 1, sums[1], F32(0)))
     rounds = (
         (c, ((sib, 1 - c),)),
@@ -536,30 +588,33 @@
 
     pv_send(0)
     for n, s in enumerate((2, 1, 0)):
-        gather_step(1, s)
+        for pt in range(2):
+            gather_step(2, s, pt)
         pv_sum(n)
         pv_send(n + 1)
     for k in range(8):
         for cp in o_copy(k, c):
             cp.start()
-    for g in range(2):
-        for s in (3, 2, 1, 0):
+    for g in range(CHUNKS):
+        for s in (3, *reversed(range(len(STEPS[g])))):
             for qi in range(4):
-                fw_copy(g, qi, s, 1 - c).wait_recv()
+                for pt in range(len(PARTS[g])):
+                    fw_copy(g, qi, s, 1 - c, pt).wait_recv()
     for k in range(8):
         for cp in o_copy(k, 1 - c):
             cp.start()
     pv_sum(3)
     proj_out[...] = pvs[4]
-    for g in range(2):
+    for g in range(CHUNKS):
         for qi in range(4):
-            for s in range(3):
-                rs_copy(g, qi, s).wait_send()
-                ag_copy(g, qi, s, True).wait_send()
-            for s in range(4):
-                fw_copy(g, qi, s, c).wait_send()
-            if CELLS[g][qi][0] == 1:
-                x_copy(g, qi).wait_send()
+            for pt in range(len(PARTS[g])):
+                for s in range(len(STEPS[g])):
+                    rs_copy(g, qi, s, pt).wait_send()
+                    ag_copy(g, qi, s, True, pt).wait_send()
+                    fw_copy(g, qi, s, c, pt).wait_send()
+                fw_copy(g, qi, 3, c, pt).wait_send()
+                if CELLS[g][qi][0] == 1:
+                    x_copy(g, qi, pt).wait_send()
     for m in range(NC):
         ls_copy(m).wait_send()
         ro_copy(m).wait_send()
@@ -574,7 +629,7 @@
                 cp.wait()
 
 
-def compact_body(rstart, rsize, src, out):
+def compact_body(rstart, rsize, proj, src, out, proj_out):
     x = lax.axis_index("site")
     k = pl.program_id(0)
     x_l = x + 1 - 2 * (x % 2)
@@ -582,18 +637,21 @@
     @pl.when(k == 0)
     def _():
         out[...] = jnp.zeros_like(out)
+        for i in range(2):
+            proj_out[i] = proj[0, i]
 
     xt = jnp.where(k // 4 == 0, x, x_l)
     site = xt + ((k // 2) % 2) * (3 - 2 * xt)
     q = site * 4 + 2 * (k % 2)
     start = rstart[q]
     base = pl.multiple_of(jnp.minimum((start // 128) * 128, BOND - 512), 128)
-    j = iota((384, 512), 0)
+    j = iota((384, 1), 0)
     odd = j >= W
     idx = jnp.where(odd, j - W, j)
     size = jnp.where(odd, rsize[q + 1], rsize[q])
     first = jnp.where(odd, rstart[q + 1], start) - base
-    hot = one_hot((idx < size) & (iota((384, 512), 1) == idx + first))
+    target = jnp.where(idx < size, idx + first, -1)
+    hot = one_hot(iota((384, 512), 1) == target)
     out[:, pl.ds(base, 512)] += jnp.dot(src[0], hot, preferred_element_type=F32).astype(BF)
 
 
@@ -625,37 +683,38 @@
             pltpu.VMEM((5, SLOTS, 3, W, 128), BF),
             pltpu.VMEM((4, 2, SLOTS, 3, 320, 128), BF),
             pltpu.VMEM((768, NS * 256), BF),
-            pltpu.VMEM((2, 4, 384, 384), F32),
-            pltpu.VMEM((8, 2, 48, BOND), BF),
-            pltpu.VMEM((8, 48, 384), F32),
-            pltpu.VMEM((8, 2, 48, 384), F32),
-            pltpu.VMEM((2, 4, 192, 384), F32),
-            pltpu.VMEM((2, 4, 96, 384), F32),
+            pltpu.VMEM((16, W, 384), F32),
+            pltpu.VMEM((12, 2, 48, BOND), BF),
+            pltpu.VMEM((12, 48, 384), F32),
+            pltpu.VMEM((12, 2, 48, 384), F32),
+            pltpu.VMEM((4, 192, 384), F32),
+            pltpu.VMEM((3, 4, 96, 384), F32),
+            pltpu.VMEM((3, 4, 48, 384), F32),
+            pltpu.VMEM((3, 4, 48, 384), F32),
             pltpu.VMEM((2, 4, 48, 384), F32),
-            pltpu.VMEM((2, 4, 48, 384), F32),
-            pltpu.VMEM((2, 4, 48, 384), F32),
+            pltpu.VMEM((3, 4, 48, 384), F32),
             pltpu.VMEM((5, 8, 128), F32),
             pltpu.VMEM((4, 4, 8, 128), F32),
-            dma((2, 2)), dma, dma((8, 2)), dma((8, 2, 2)),
+            dma((2, 2)), dma, dma((12, 2)), dma((8, 2, 2)),
             dma((2, NC, 2)), dma((2, NC, 2)), dma((NC,)), dma((NC,)), dma((2, NC)), dma((2, NC)),
             dma((NC,)), dma((NC,)), dma((2, NC)), dma((2, NC)),
-            dma((2, 4, 4)), dma((2, 4, 4)), dma((2, 4)), dma((2, 4)),
-            dma((2, 4, 3)), dma((2, 4, 3)), dma((2, 4, 4)), dma((2, 4, 4)), dma((4, 3)), dma((4, 4)),
+            dma((3, 4, 4, 2)), dma((3, 4, 4, 2)), dma((3, 4, 2)), dma((3, 4, 2)),
+            dma((3, 4, 3, 2)), dma((3, 4, 3, 2)), dma((3, 4, 4, 2)), dma((3, 4, 4, 2)), dma((4, 3)), dma((4, 4)),
         ],
         compiler_params=pltpu.CompilerParams(
             collective_id=0, has_side_effects=True, vmem_limit_bytes=67043328),
         name="exchange",
     )(lstart, lsize, rstart, rsize, term_count, wavefunction.reshape(BOND // 16, 16, BOND),
       left_blocks, right_blocks, left_energy.reshape(16, 1, 128), right_energy.reshape(1, BOND), subspace)
-    sigma = pl.pallas_call(
+    sigma, projections = pl.pallas_call(
         compact_body,
         grid=(8,),
-        out_shape=jax.ShapeDtypeStruct((768, BOND), BF),
-        in_specs=[smem, smem, pl.BlockSpec((1, 768, 384), lambda k: (k, 0, 0))],
-        out_specs=pl.BlockSpec((768, BOND), lambda k: (0, 0)),
+        out_shape=(jax.ShapeDtypeStruct((768, BOND), BF), jax.ShapeDtypeStruct((2,), F32)),
+        in_specs=[smem, smem, smem, pl.BlockSpec((1, 768, 384), lambda k: (k, 0, 0))],
+        out_specs=(pl.BlockSpec((768, BOND), lambda k: (0, 0)), smem),
         name="compact",
-    )(rstart, rsize, slabs.reshape(8, 768, 384))
-    return sigma.reshape(4, W, BOND), proj[0, :2]
+    )(rstart, rsize, proj, slabs.reshape(8, 768, 384))
+    return sigma.reshape(4, W, BOND), projections
 
 
 def solution(mesh):

time: 136 us -> 128 us (0.941)
  Pallas kernels: 132 us -> 125 us
    pallas_call x1, Pallas kernels: 122 us -> 115 us  [local(): pl.pallas_call(body, out_shape=(jax.ShapeDtypeStruct((8, 48, 16, 384), BF...]
where the time goes in v5:
time: 128 us
  Pallas kernels  125 us (98%)
  other arithmetic  1.49 us (1%)
  between operations  1.47 us (1%)
    pallas_call x1, Pallas kernels, local(): pl.pallas_call(body, out_shape=(jax.ShapeDtypeStruct((8, 48, 16, 384), BF...  115 us
    pallas_call x1, Pallas kernels, local(): pl.pallas_call(compact_body, grid=(8,), out_shape=(jax.ShapeDtypeStruct((...  9.51 us

profile of v5, /device:TPU:1, one launch (start us, length us, event | category | flops | bytes accessed | tf_op | source)
XLA Modules:
  0.0 127.8 jit_solution(2718685563322727084)
XLA Ops:
  1.3 1.5 %convert_reduce_fusion = (s32[16]{0:T(128)}, s32[16]{0:T(128)}, s32[16]{0:T(128)}, s32[16]{0:T(128)}) fusion(s32[2048]{0:T(1024)} %param.12, s32[2048]{0:T(1024)} %param.13), kind=kLoop, calls=%fused_computation | loop fusion | flops 393152 | bytes 16640 | tf_op jit(solution)/shard_map/reduce_sum | solution.py:661
  2.8 115.4 %exchange.1 = (bf16[8,48,16,384]{3,2,1,0:T(8,128)(2,1)}, f32[8,128]{1,0:T(8,128)}) custom-call(s32[16]{0:T(128)} %get-tuple-element.11.lstart, s32[16]{0:T(128)} %get-tuple-element.10.lsize, s32[16]{0:T(128)} %get-tuple-element.14.rstart, s32[16]{0:T(128)} %get-tuple-element.15.rsize, s32[1]{0:T(128)S(6)} %copy.11.count, bf16[128,16,2048]{2,1,0:T(8,128)(2,1)} %bitcast.5, ...), custom_call_target="tpu_custom_call" | custom-call | tf_op jit(solution)/shard_map/exchange/pallas_call | solution.py:673
  118.2 9.5 %compact.1 = (bf16[768,2048]{1,0:T(8,128)(2,1)}, f32[2]{0:T(128)}) custom-call(s32[16]{0:T(128)} %get-tuple-element.14.rstart, s32[16]{0:T(128)} %get-tuple-element.15.rsize, f32[8,128]{1,0:T(8,128)} %get-tuple-element.6.proj, bf16[8,768,384]{2,1,0:T(8,128)(2,1)} %bitcast.6), custom_call_target="tpu_custom_call" | custom-call | tf_op jit(solution)/shard_map/compact/pallas_call | solution.py:709

commit v6 on v5

--- a/solution.py
+++ b/solution.py
@@ -631,28 +631,30 @@
 
 def compact_body(rstart, rsize, proj, src, out, proj_out):
     x = lax.axis_index("site")
-    k = pl.program_id(0)
+    step = pl.program_id(0)
     x_l = x + 1 - 2 * (x % 2)
 
-    @pl.when(k == 0)
+    @pl.when(step == 0)
     def _():
         out[...] = jnp.zeros_like(out)
         for i in range(2):
             proj_out[i] = proj[0, i]
 
-    xt = jnp.where(k // 4 == 0, x, x_l)
-    site = xt + ((k // 2) % 2) * (3 - 2 * xt)
-    q = site * 4 + 2 * (k % 2)
-    start = rstart[q]
-    base = pl.multiple_of(jnp.minimum((start // 128) * 128, BOND - 512), 128)
-    j = iota((384, 1), 0)
-    odd = j >= W
-    idx = jnp.where(odd, j - W, j)
-    size = jnp.where(odd, rsize[q + 1], rsize[q])
-    first = jnp.where(odd, rstart[q + 1], start) - base
-    target = jnp.where(idx < size, idx + first, -1)
-    hot = one_hot(iota((384, 512), 1) == target)
-    out[:, pl.ds(base, 512)] += jnp.dot(src[0], hot, preferred_element_type=F32).astype(BF)
+    for n in range(4):
+        k = step * 4 + n
+        xt = jnp.where(k // 4 == 0, x, x_l)
+        site = xt + ((k // 2) % 2) * (3 - 2 * xt)
+        q = site * 4 + 2 * (k % 2)
+        start = rstart[q]
+        base = pl.multiple_of(jnp.minimum((start // 128) * 128, BOND - 512), 128)
+        j = iota((384, 1), 0)
+        odd = j >= W
+        idx = jnp.where(odd, j - W, j)
+        size = jnp.where(odd, rsize[q + 1], rsize[q])
+        first = jnp.where(odd, rstart[q + 1], start) - base
+        target = jnp.where(idx < size, idx + first, -1)
+        hot = one_hot(iota((384, 512), 1) == target)
+        out[:, pl.ds(base, 512)] += jnp.dot(src[n], hot, preferred_element_type=F32).astype(BF)
 
 
 def sector_tables(sector_ids, sectors):
@@ -708,9 +710,9 @@
       left_blocks, right_blocks, left_energy.reshape(16, 1, 128), right_energy.reshape(1, BOND), subspace)
     sigma, projections = pl.pallas_call(
         compact_body,
-        grid=(8,),
+        grid=(2,),
         out_shape=(jax.ShapeDtypeStruct((768, BOND), BF), jax.ShapeDtypeStruct((2,), F32)),
-        in_specs=[smem, smem, smem, pl.BlockSpec((1, 768, 384), lambda k: (k, 0, 0))],
+        in_specs=[smem, smem, smem, pl.BlockSpec((4, 768, 384), lambda k: (k, 0, 0))],
         out_specs=(pl.BlockSpec((768, BOND), lambda k: (0, 0)), smem),
         name="compact",
     )(rstart, rsize, proj, slabs.reshape(8, 768, 384))

time: 128 us -> 126 us (0.984)
  Pallas kernels: 125 us -> 123 us
    pallas_call x1, Pallas kernels: 9.51 us -> 7.31 us  [local(): pl.pallas_call(compact_body, grid=(2,), out_shape=(jax.ShapeDtypeStruct((...]
where the time goes in v6:
time: 126 us
  Pallas kernels  123 us (98%)
  other arithmetic  1.49 us (1%)
  between operations  1.47 us (1%)
    pallas_call x1, Pallas kernels, local(): pl.pallas_call(body, out_shape=(jax.ShapeDtypeStruct((8, 48, 16, 384), BF...  115 us
    pallas_call x1, Pallas kernels, local(): pl.pallas_call(compact_body, grid=(2,), out_shape=(jax.ShapeDtypeStruct((...  7.31 us

profile of v6, /device:TPU:1, one launch (start us, length us, event | category | flops | bytes accessed | tf_op | source)
XLA Modules:
  0.0 125.6 jit_solution(15287526503932485861)
XLA Ops:
  1.3 1.5 %convert_reduce_fusion = (s32[16]{0:T(128)}, s32[16]{0:T(128)}, s32[16]{0:T(128)}, s32[16]{0:T(128)}) fusion(s32[2048]{0:T(1024)} %param.12, s32[2048]{0:T(1024)} %param.13), kind=kLoop, calls=%fused_computation | loop fusion | flops 393152 | bytes 16640 | tf_op jit(solution)/shard_map/reduce_sum | solution.py:663
  2.8 115.4 %exchange.1 = (bf16[8,48,16,384]{3,2,1,0:T(8,128)(2,1)}, f32[8,128]{1,0:T(8,128)}) custom-call(s32[16]{0:T(128)} %get-tuple-element.11.lstart, s32[16]{0:T(128)} %get-tuple-element.10.lsize, s32[16]{0:T(128)} %get-tuple-element.14.rstart, s32[16]{0:T(128)} %get-tuple-element.15.rsize, s32[1]{0:T(128)S(6)} %copy.11.count, bf16[128,16,2048]{2,1,0:T(8,128)(2,1)} %bitcast.5, ...), custom_call_target="tpu_custom_call" | custom-call | tf_op jit(solution)/shard_map/exchange/pallas_call | solution.py:675
  118.2 7.3 %compact.1 = (bf16[768,2048]{1,0:T(8,128)(2,1)}, f32[2]{0:T(128)}) custom-call(s32[16]{0:T(128)} %get-tuple-element.14.rstart, s32[16]{0:T(128)} %get-tuple-element.15.rsize, f32[8,128]{1,0:T(8,128)} %get-tuple-element.6.proj, bf16[8,768,384]{2,1,0:T(8,128)(2,1)} %bitcast.6), custom_call_target="tpu_custom_call" | custom-call | tf_op jit(solution)/shard_map/compact/pallas_call | solution.py:711
